TPU v7x, 1024 devices: a whole 4x8x16 slice. The times are simulated.
1024 devices in a mesh: dp: 64 (over x_hi, z, core), tensor: 16 (over x_lo, y).
Axes of the slice: x: 4 (x_hi: 2, x_lo: 2; x = x_hi * 2 + x_lo), y: 8, z: 16, core: 2. Of those that a mesh axis runs over, the one named last changes fastest.
Arguments:
- block_input: bfloat16 [16384, 5120], P('dp'), may hold values from -16 to 16
- query_weight: bfloat16 [2560, 5120], P('tensor'), as said below
- query_gain: float32 [2560], P('tensor'), may hold values from 0.5 to 2
- query_grad: bfloat16 [2560, 16384], P('tensor', 'dp'), may hold values from -6 to 6
Outputs:
- input_grad: bfloat16 [16384, 5120], P(('dp', 'tensor'))
- weight_grad: float32 [5120, 2560], P('dp', 'tensor')
Inputs may be any that keep to these rules, and one draw needn't show every extreme that they name: `query_weight`: entries are normal with standard deviation 5120 ** -0.5 times a factor between 0.25 and 75, which may differ from row to row and from column to column.
All inputs are finite; a program needn't handle non-finite values.
Results may differ from a plain program's by a relative error of at most 0.017.
Values may be sent and summed in bfloat16 or wider, within the bound.
A program may use at most 64 MiB of HBM per device.

v0:
```python
import jax
import jax.numpy as jnp
from jax import lax
from jax.sharding import Mesh
from jax.sharding import PartitionSpec as P

DP = ("dp_0", "dp_1", "dp_2")
DP_TENSOR = ("dp_0", "dp_1", "dp_2", "tensor")


epsilon = 1e-06


def sent_to_all(x, axis):
    size = lax.axis_size(axis)
    return lax.all_to_all(jnp.broadcast_to(x[None], (size, *x.shape)), axis, 0, 0, tiled=True)


def of_everyone(x, axis):
    return sent_to_all(x, axis).sum(axis=0)


def together(arrays, axis):
    line, at, done = (jnp.concatenate([a.reshape(-1) for a in arrays]), 0, [])
    running = of_everyone(line, axis)
    for a in arrays:
        done.append(running[at : at + a.size].reshape(a.shape))
        at += a.size
    return tuple(done)


def split_up(x, dim, size):
    dims = x.shape
    tiles = x.reshape(*dims[:dim], size, dims[dim] // size, *dims[dim + 1 :])
    return jnp.moveaxis(tiles, dim, 0)


def sent_and_summed(x, axis, dim):
    tiles = split_up(x, dim, lax.axis_size(axis))
    arrived = lax.all_to_all(tiles, axis, split_axis=0, concat_axis=0, tiled=True)
    return arrived.astype(jnp.float32).sum(axis=0)


def reduced_to_own(tiles, axes, order):
    inside = tiles.shape[1:]
    tiles = tiles.reshape(*(lax.axis_size(a) for a in axes), *inside)
    tiles = jnp.moveaxis(tiles, order, range(len(axes))).reshape(-1, *inside)
    for k in order:
        tiles = lax.psum_scatter(tiles, axes[k], scatter_dimension=0, tiled=True)
    return tiles[0]


def scatter_axes(x, axes, order, dim):
    size = lax.axis_size(axes)
    return reduced_to_own(split_up(x, dim, size), axes, order)


def per_device(block_input, query_weight, query_gain, query_grad):
    projected = lax.dot_general(
        query_weight, block_input, (((1,), (1,)), ((), ())), preferred_element_type=jnp.float32
    )
    scaled_grad = query_grad.astype(jnp.float32) * query_gain[:, None]
    squares = jnp.sum(projected * projected, axis=0)
    cross_sums = jnp.sum(scaled_grad * projected, axis=0)
    features = query_gain.shape[0] * lax.axis_size("tensor")
    squares, cross_sums = together((squares, cross_sums), "tensor")
    inverse_rms = 1.0 / jnp.sqrt(squares / features + epsilon)
    coefficient = inverse_rms * inverse_rms * inverse_rms * (cross_sums / features)
    proj_grad = (inverse_rms[None, :] * scaled_grad - coefficient[None, :] * projected).astype(
        jnp.bfloat16
    )
    columns = proj_grad
    input_grad = sent_and_summed(
        lax.dot_general(
            columns, query_weight, (((0,), (0,)), ((), ())), preferred_element_type=jnp.float32
        ).astype(jnp.bfloat16),
        "tensor",
        0,
    ).astype(jnp.bfloat16)
    columns = block_input
    weight_grad = scatter_axes(
        lax.dot_general(
            columns, proj_grad, (((0,), (1,)), ((), ())), preferred_element_type=jnp.float32
        ),
        DP,
        (2, 1, 0),
        0,
    )
    return (input_grad, weight_grad)


def solution(mesh):
    split = Mesh(
        mesh.devices.reshape(2, 16, 2, mesh.shape["tensor"]), ("dp_0", "dp_1", "dp_2", "tensor")
    )
    return jax.shard_map(
        per_device,
        mesh=split,
        in_specs=(P(DP, None), P("tensor", None), P("tensor"), P("tensor", DP)),
        out_specs=(P(DP_TENSOR, None), P(DP, "tensor")),
        check_vma=False,
    )
```

profile of v0, /device:TPU:1, one launch (start us, length us, event | category | flops | bytes accessed | tf_op | source)
XLA Modules:
  0.0 199.3 jit_solution(7362582667188248365)
XLA Ops:
  7.2 0.0 copy-start
  7.2 0.0 copy-start.2
  7.2 0.0 copy-start.1
  7.2 0.0 reduce-scatter.4.cloned.1.call-start
  7.2 1.7 copy-done
  8.9 2.5 %multiply_reduce_fusion.1 = (f32[256]{0:T(256)S(1)}, f32[256]{0:T(256)S(1)}, f32[160,256]{1,0:T(8,128)S(1)}) fusion(f32[160]{0:T(256)} %param.6, bf16[160,256]{1,0:T(8,128)(2,1)} %param.7, bf16[160,5120]{1,0:T(8,128)(2,1)} %param.5, bf16[256,5120]{1,0:T(8,128)(2,1)S(1)} %copy-done), kind=kOutput, calls=%fused_computation.5 | convolution fusion | flops 419675648 | bytes 4508288 | tf_op jit(solution)/shard_map/dot_general | solution.py:59
  11.4 15.8 %all_to_all.11 = f32[16,1,512]{2,1,0:T(1,128)S(1)} all-to-all(f32[16,1,512]{2,1,0:T(1,128)S(1)} %broadcast_in_dim.2), channel_id=1, replica_groups=mesh['dp_0'=2,'dp_1'=16,'dp_2'=2,'tensor'=16] {'tensor'}, dimensions={0} | all-to-all | bytes 65536 | tf_op jit(solution)/shard_map/all_to_all | solution.py:16
  27.3 0.0 copy-done.2
  27.3 0.1 subtract_convert_fusion
  27.4 2.3 %convolution_bitcast_fusion = f32[5120,160]{0,1:T(8,128)} fusion(bf16[160,256]{1,0:T(8,128)(2,1)S(1)} %subtract_convert_fusion, bf16[256,5120]{1,0:T(8,128)(2,1)S(1)} %copy-done), kind=kOutput, calls=%fused_computation.1 | convolution fusion | flops 419430400 | bytes 5980160 | tf_op jit(solution)/shard_map/dot_general | solution.py:82
  29.7 12.0 %reshape_reshape.3 = f32[2,16,2,80,160]{3,2,1,0,4:T(2,128)} reshape(f32[5120,160]{0,1:T(8,128)} %convolution_bitcast_fusion) | data formatting | bytes 6553600 | tf_op jit(solution)/shard_map/reshape;reshape | solution.py:46
  41.7 10.3 %copy.9 = f32[2,16,2,80,160]{4,3,2,1,0:T(8,128)} copy(f32[2,16,2,80,160]{3,0,1,2,4:T(2,128)} %bitcast.15) | data formatting | bytes 6553600 | tf_op jit(solution)/shard_map/transpose | solution.py:47
  52.0 0.0 reduce-scatter.4.cloned.1.call-update
  52.0 3.8 %convolution_convert_fusion = bf16[256,5120]{1,0:T(8,128)(2,1)} fusion(bf16[160,256]{1,0:T(8,128)(2,1)S(1)} %subtract_convert_fusion, bf16[160,5120]{1,0:T(8,128)(2,1)} %param.5), kind=kOutput, calls=%fused_computation | convolution fusion | flops 420741120 | bytes 4341760 | tf_op jit(solution)/shard_map/dot_general | solution.py:74
  55.8 4.4 %all-to-all-start.1 = ((bf16[16,16,5120]{2,1,0:T(8,128)(2,1)}), bf16[16,16,5120]{2,1,0:T(8,128)(2,1)}, u32[]{:S(2)}, u32[]{:S(2)}) async-start(bf16[16,16,5120]{2,1,0:T(8,128)(2,1)} %bitcast.16), calls=%async_computation.1 | async-start | bytes 5242880 | tf_op jit(solution)/shard_map/all_to_all | solution.py:40
  60.3 0.0 reduce-scatter.6.cloned.1.call-start
  60.3 24.5 %reduce-scatter.4.cloned.1.call-done = f32[32,80,160]{2,1,0:T(8,128)} async-done(((f32[64,80,160]{2,1,0:T(8,128)}), f32[32,80,160]{2,1,0:T(8,128)}) %reduce-scatter.4.cloned.1.call-update) | async-done | bytes 1638416 | tf_op jit(solution)/shard_map/reduce_scatter | solution.py:49
  84.8 0.0 reduce-scatter.6.cloned.1.call-update
  84.9 0.0 reduce-scatter.8.cloned.1.call-start
  84.9 72.9 %reduce-scatter.6.cloned.1.call-done = f32[2,80,160]{2,1,0:T(8,128)} async-done(((f32[32,80,160]{2,1,0:T(8,128)}), f32[2,80,160]{2,1,0:T(8,128)}) %reduce-scatter.6.cloned.1.call-update) | async-done | bytes 102416 | tf_op jit(solution)/shard_map/reduce_scatter | solution.py:49
  157.8 0.0 reduce-scatter.8.cloned.1.call-update
  157.8 0.0 all-to-all-done.1
  157.8 2.8 %reduce_sum.42 = bf16[16,5120]{1,0:T(8,128)(2,1)} reduce(bf16[16,16,5120]{2,1,0:T(8,128)(2,1)} %all-to-all-done.1, bf16[]{:T(256)} %constant.10.clone.1), dimensions={0}, to_apply=%region_3.0 | reduce | flops 1228800 | bytes 2785282 | tf_op jit(solution)/shard_map/reduce_sum | solution.py:41
  160.7 32.2 %reduce-scatter.8.cloned.1.call-done = f32[1,80,160]{2,1,0:T(8,128)} async-done(((f32[2,80,160]{2,1,0:T(8,128)}), f32[1,80,160]{2,1,0:T(8,128)}) %reduce-scatter.8.cloned.1.call-update) | async-done | bytes 51216 | tf_op jit(solution)/shard_map/reduce_scatter | solution.py:49
  (5 shorter events, 0.1 us)
Async XLA Ops:
  7.2 1.7 copy-start
  7.2 20.1 %copy-start.2 = (f32[160]{0:T(256)S(1)}, f32[160]{0:T(256)}, u32[]{:S(2)}) copy-start(f32[160]{0:T(256)} %param.6) | copy-start | bytes 1924
  7.2 20.1 %copy-start.1 = (bf16[160,256]{1,0:T(8,128)(2,1)S(1)}, bf16[160,256]{1,0:T(8,128)(2,1)}, u32[]{:S(2)}) copy-start(bf16[160,256]{1,0:T(8,128)(2,1)} %param.7) | copy-start | bytes 245764
  7.2 77.6 %reduce-scatter.4.cloned.1.call-start = ((), (), s32[]{:S(2)}) async-start(), calls=%async_computation.5 | async-start | bytes 7864320 | tf_op jit(solution)/shard_map/reduce_scatter | solution.py:49
  55.8 102.0 %all-to-all-start.1 = ((bf16[16,16,5120]{2,1,0:T(8,128)(2,1)}), bf16[16,16,5120]{2,1,0:T(8,128)(2,1)}, u32[]{:S(2)}, u32[]{:S(2)}) async-start(bf16[16,16,5120]{2,1,0:T(8,128)(2,1)} %bitcast.16), calls=%async_computation.1 | async-start | bytes 5242880 | tf_op jit(solution)/shard_map/all_to_all | solution.py:40
  60.3 97.5 %reduce-scatter.6.cloned.1.call-start = ((), (), s32[]{:S(2)}) async-start(), calls=%async_computation.6 | async-start | bytes 2785280 | tf_op jit(solution)/shard_map/reduce_scatter | solution.py:49
  84.9 107.9 %reduce-scatter.8.cloned.1.call-start = ((), (), s32[]{:S(2)}) async-start(), calls=%async_computation.7 | async-start | bytes 245760 | tf_op jit(solution)/shard_map/reduce_scatter | solution.py:49
Sparse Core Ops, SparseCore 0:
  52.1 32.6 reduce-scatter.3
  88.2 69.5 reduce-scatter.5
  161.7 31.0 reduce-scatter.7
where the time goes:
time: 200 us; the launch traced here: 199 us
  waiting for transfers between devices  130 us (65%)
  local copies, waits for them, and re-layouts  24 us (12%)
  blocking collectives  15.8 us (8%)
  between operations  13.8 us (7%)
  matrix products  8.58 us (4%)
  starting transfers between devices  4.56 us (2%)
  other arithmetic  2.98 us (1%)
    reduce_scatter x3, waiting for transfers between devices, reduced_to_own(): tiles = lax.psum_scatter(tiles, axes[k], scatter_dimension=0, tiled=True)  130 us
    all_to_all x1, blocking collectives, sent_to_all(): lax.all_to_all(jnp.broadcast_to(x[None], (size, *x.shape)), axis, 0, 0, t...  15.8 us
    another operation x1, local copies, waits for them, and re-layouts, reduced_to_own(): tiles = tiles.reshape(*(lax.axis_size(a) for a in axes), *inside)  12 us
    transpose x1, local copies, waits for them, and re-layouts, reduced_to_own(): tiles = jnp.moveaxis(tiles, order, range(len(axes))).reshape(-1, *inside)  10.3 us
    all_to_all x1, starting transfers between devices, sent_and_summed(): lax.all_to_all(tiles, axis, split_axis=0, concat_axis=0, tiled=True)  4.45 us
  transfers between devices with their start and end apart: 4, of which 3 were waited for; matrix products, arithmetic and copies ran while one was open for 3% of the time, Pallas kernels for 0%

commit v1 on v0

v1 whole, which is shorter than its diff:
```python
import jax
import jax.numpy as jnp
from jax import lax
from jax.experimental import pallas as pl
from jax.experimental.pallas import tpu as pltpu
from jax.sharding import PartitionSpec as P

MESH = pl.DeviceIdType.MESH
F32, BF16 = jnp.float32, jnp.bfloat16

NT, NY, NZ = 16, 8, 16
T, F, D = 256, 160, 5120
HALF = D // 2
S = 4
CS = HALF // S
KC = 4
KW = D // KC
HQ = F * NT
epsilon = 1e-6

STEPS = ((8, 4, -7, -4), (7, 3, -6, -3), (6, 2, -5, -2), (5, 1, -1, 0))
LAST = {5: 0, 1: 1, -5: 2, -1: 3}
HEADS = (8, 4, -7, -4)
YSTEPS = ((4, -3), (3, -2), (2, -1), (1,))
YHEADS = (4, -3)

SUMS = 0
WX = SUMS + NT
WD = WX + 4
PG = WD + 4
DD = PG + 1
ZC = DD + 4
FIN = ZC + 16
YC = FIN + 9
YF = YC + 8 * S
NSEM = YF + S


def dot(a, b, dims):
    return lax.dot_general(a, b, (dims, ((), ())), preferred_element_type=F32)


def kernel(
    x_hbm, w_hbm, gain_ref, qg_hbm, ig_hbm, wg_hbm,
    x_v, xt_v, w_v, wh_v, wp_v, qg_v, sums_v, pga_v, pgb_v, pgp_v,
    dsend, drecv, own_v, zsend, zrecv, fin_v, wg_v,
    part_v, ysend, yrecv, yfin, yfinr,
    lsem, ssem, rsem,
):
    d = lax.axis_index("dp")
    t = lax.axis_index("tensor")
    core = lax.rem(d, 2)
    z = lax.rem(lax.div(d, 2), NZ)
    xh = lax.div(d, 2 * NZ)
    y = lax.rem(t, NY)
    xl = lax.div(t, NY)
    sgn = 1 - 2 * core

    def dev(xh_, z_, core_, xl_, y_):
        return {"dp": (xh_ * NZ + z_) * 2 + core_, "tensor": xl_ * NY + y_}

    def zat(r):
        return lax.rem(z + sgn * r + 2 * NZ, NZ)

    def yat(r):
        return lax.rem(y + sgn * r + 2 * NY, NY)

    sibling = dev(xh, z, 1 - core, xl, y)
    partner = dev(xh, z, core, 1 - xl, y)
    across = dev(1 - xh, z, core, 1 - xl, y)

    loads = []
    for k in range(KC):
        cols = pl.ds(k * KW, KW)
        loads.append((
            pltpu.make_async_copy(x_hbm.at[:, cols], x_v.at[:, cols], lsem.at[k]),
            pltpu.make_async_copy(w_hbm.at[:, cols], w_v.at[:, cols], lsem.at[KC + k]),
        ))
    for a, b in loads:
        a.start()
        b.start()
    qg_load = pltpu.make_async_copy(qg_hbm, qg_v, lsem.at[2 * KC])
    qg_load.start()
    myhalf = pl.ds(pl.multiple_of(xl * HALF, 128), HALF)
    wh_load = pltpu.make_async_copy(w_hbm.at[:, myhalf], wh_v, lsem.at[2 * KC + 1])
    wh_load.start()

    barrier = pltpu.get_barrier_semaphore()
    peers = [{"dp": d, "tensor": lax.rem(t + o, NT)} for o in range(1, NT)]
    peers += [across, sibling]
    peers += [dev(xh, zat(r), core, xl, y) for r in (1, -1, 5, -5)]
    peers += [dev(1 - xh, zat(r), core, xl, y) for r in (1, -1, 5, -5, 0)]
    for p in peers:
        pl.semaphore_signal(barrier, inc=1, device_id=p, device_id_type=MESH)

    pt = None
    for k, (a, b) in enumerate(loads):
        a.wait()
        b.wait()
        cols = slice(k * KW, (k + 1) * KW)
        term = dot(w_v[:, cols], x_v[:, cols], ((1,), (1,)))
        pt = term if pt is None else pt + term
    qg_load.wait()
    rows = lax.broadcasted_iota(jnp.int32, (F, F), 0)
    lanes = lax.broadcasted_iota(jnp.int32, (F, F), 1)
    gain = jnp.sum(jnp.where(rows == lanes, gain_ref[...], 0.0), axis=1, keepdims=True)
    sg = qg_v[...].astype(F32) * gain
    sq = jnp.sum(pt * pt, axis=0, keepdims=True)
    cr = jnp.sum(sg * pt, axis=0, keepdims=True)
    sums_v[t, 0:1, :] = sq[:, :128]
    sums_v[t, 1:2, :] = sq[:, 128:]
    sums_v[t, 2:3, :] = cr[:, :128]
    sums_v[t, 3:4, :] = cr[:, 128:]

    pl.semaphore_wait(barrier, len(peers))

    started = []

    def send(src, dst, index, device):
        copy = pltpu.make_async_remote_copy(
            src_ref=src, dst_ref=dst, send_sem=ssem.at[index], recv_sem=rsem.at[index],
            device_id=device, device_id_type=MESH,
        )
        copy.start()
        started.append(copy)

    def arrived(dst, index):
        pltpu.make_async_remote_copy(
            src_ref=dst, dst_ref=dst, send_sem=ssem.at[index], recv_sem=rsem.at[index],
            device_id=sibling, device_id_type=MESH,
        ).wait_recv()

    for o in range(1, NT):
        copy = pltpu.make_async_remote_copy(
            src_ref=sums_v.at[t], dst_ref=sums_v.at[t],
            send_sem=ssem.at[SUMS + o], recv_sem=rsem.at[SUMS + t],
            device_id=peers[o - 1], device_id_type=MESH,
        )
        copy.start()
        started.append(copy)

    for n, who in enumerate((partner, across)):
        src = pl.ds(pl.multiple_of((1 - xl) * HALF + (2 * n + core) * CS, 128), CS)
        dst = pl.ds(pl.multiple_of((2 * n + core) * CS, 128), CS)
        send(w_v.at[:, src], wp_v.at[:, dst], WX + n, who)

    for k in range(D // 256):
        xt_v[k * 256 : (k + 1) * 256, :] = x_v[:, k * 256 : (k + 1) * 256].T
    pga_v[F:, :] = jnp.zeros((256 - F, T), BF16)
    pgb_v[128:160, :] = jnp.zeros((32, T), BF16)
    pgb_v[192:, :] = jnp.zeros((64, T), BF16)

    for o in range(1, NT):
        s = lax.rem(t + o, NT)
        arrived(sums_v.at[s], SUMS + s)
    total = sums_v[0]
    for s in range(1, NT):
        total = total + sums_v[s]
    sq = jnp.concatenate([total[0:1], total[1:2]], axis=1)
    cr = jnp.concatenate([total[2:3], total[3:4]], axis=1)
    inv = 1.0 / jnp.sqrt(sq / HQ + epsilon)
    coef = inv * inv * inv * (cr / HQ)
    pg = (inv * sg - coef * pt).astype(BF16)
    pga_v[:F, :] = pg
    pgb_v[:128, :] = pg[:128]
    pgb_v[160:192, :] = pg[128:]
    send(pga_v.at[:F], pgp_v, PG, partner)

    def block(dest, who):
        out = []
        for h, rhs in ((0, pga_v), (1, pgb_v)):
            at = pl.multiple_of(h * HALF + dest * 160 + who * 80, 16)
            out.append(dot(xt_v[pl.ds(at, 80), :], rhs[...], ((1,), (1,))))
        return out[0][:, :128], out[0][:, 128:] + out[1][:, 128:], out[1][:, :128]

    def blocks(g):
        for i, r in enumerate(STEPS[g]):
            for j, v in enumerate(block(lax.rem(z - sgn * r + 2 * NZ, NZ), 1 - core)):
                dsend[g, i, j * 80 : (j + 1) * 80, :] = v.astype(BF16)
        send(dsend.at[g], drecv.at[g], DD + g, sibling)
        for i, r in enumerate(STEPS[g]):
            for j, v in enumerate(block(zat(r), core)):
                own_v[g, i, j * 80 : (j + 1) * 80, :] = v

    def zstep(g):
        arrived(drecv.at[g], DD + g)
        for i, r in enumerate(STEPS[g]):
            if r not in HEADS and r != 0:
                arrived(zrecv.at[r % NZ], ZC + r % NZ)
            v = own_v[g, i] + drecv[g, i].astype(F32)
            if r == 0:
                own_v[g, i] = v
                zsend[0] = v.astype(BF16)
                send(
                    zsend.at[0, pl.ds(pl.multiple_of((1 - xh) * 80, 16), 160)],
                    fin_v.at[8], FIN + 8, dev(1 - xh, z, core, xl, y),
                )
                continue
            if r not in HEADS:
                v = v + zrecv[r % NZ].astype(F32)
            zsend[r % NZ] = v.astype(BF16)
            if r in LAST:
                for flag, h in ((0, xh), (1, 1 - xh)):
                    slot = LAST[r] * 2 + flag
                    send(
                        zsend.at[r % NZ, pl.ds(pl.multiple_of(h * 80, 16), 160)],
                        fin_v.at[slot], FIN + slot, dev(h, zat(r), core, xl, y),
                    )
            else:
                nxt = r - 1 if r > 0 else r + 1
                send(
                    zsend.at[r % NZ], zrecv.at[nxt % NZ], ZC + nxt % NZ,
                    dev(xh, zat(1 if r > 0 else -1), core, xl, y),
                )

    def yrows(r):
        return pl.multiple_of(yat(r) * 16, 16)

    def ystep(k, s):
        for r in YSTEPS[k]:
            at = yrows(r)
            new = [part_v[s, pl.ds(at + h * 128, 16), :] for h in (0, 1)]
            slot = (r % NY) * S + s
            if r not in YHEADS:
                arrived(yrecv.at[r % NY, s], YC + slot)
                new = [v + yrecv[r % NY, s, h * 16 : h * 16 + 16, :].astype(F32) for h, v in enumerate(new)]
            for h, v in enumerate(new):
                ysend[r % NY, s, h * 16 : h * 16 + 16, :] = v.astype(BF16)
            nxt = r - 1 if r > 0 else r + 1
            to = nxt % NY if nxt else (0 if r > 0 else 4)
            send(
                ysend.at[r % NY, s], yrecv.at[to, s], YC + to * S + s,
                dev(xh, z, core, xl, yat(1 if r > 0 else -1)),
            )

    blocks(0)
    zstep(0)
    for g in (1, 2, 3):
        blocks(g)

    for n in (0, 1):
        cols = pl.ds(pl.multiple_of((2 * n + core) * CS, 128), CS)
        arrived(wp_v.at[:, cols], WX + n)
        send(wp_v.at[:, cols], wp_v.at[:, cols], WD + n, sibling)
    wh_load.wait()
    arrived(pgp_v, PG)
    for n in (0, 1):
        cols = pl.ds(pl.multiple_of((2 * n + 1 - core) * CS, 128), CS)
        arrived(wp_v.at[:, cols], WD + n)
    for s in range(S):
        cols = slice(s * CS, (s + 1) * CS)
        part_v[s] = dot(pga_v[:F, :], wh_v[:, cols], ((0,), (0,))) + dot(
            pgp_v[...], wp_v[:, cols], ((0,), (0,))
        )
        ystep(0, s)

    for k in (1, 2, 3):
        zstep(k)
        for s in range(S):
            ystep(k, s)

    outs = []
    for s in range(S):
        arrived(yrecv.at[0, s], YC + s)
        arrived(yrecv.at[4, s], YC + 4 * S + s)
        for h in (0, 1):
            rows = slice(h * 16, h * 16 + 16)
            v = part_v[s, pl.ds(yrows(0) + h * 128, 16), :]
            v = v + yrecv[0, s, rows, :].astype(F32) + yrecv[4, s, rows, :].astype(F32)
            yfin[s, rows, :] = v.astype(BF16)
        send(
            yfin.at[s, pl.ds(pl.multiple_of((1 - xl) * 16, 16), 16)], yfinr.at[s], YF + s, partner
        )
        copy = pltpu.make_async_copy(
            yfin.at[s, pl.ds(pl.multiple_of(xl * 16, 16), 16)],
            ig_hbm.at[:, pl.ds(pl.multiple_of(xl * HALF + s * CS, 128), CS)],
            lsem.at[2 * KC + 2 + s],
        )
        copy.start()
        outs.append(copy)

    for slot in range(9):
        arrived(fin_v.at[slot], FIN + slot)
    main_at = pl.multiple_of(xh * 80, 16)
    rest_at = pl.multiple_of((1 - xh) * 80, 16)
    main = own_v[3, 3, pl.ds(pl.multiple_of(xh * 160, 16), 80), :]
    rest = own_v[3, 3, 80:160, :]
    for slot in range(9):
        main = main + fin_v[slot, pl.ds(main_at, 80), :].astype(F32)
        rest = rest + fin_v[slot, pl.ds(rest_at, 80), :].astype(F32)
    wg_v[:, :128] = main
    wg_v[:, 128:] = jnp.where(xh == 0, rest[:, :32], rest[:, 32:64])
    wg_copy = pltpu.make_async_copy(wg_v, wg_hbm, lsem.at[2 * KC + 2 + 2 * S])
    wg_copy.start()
    outs.append(wg_copy)

    for s in range(S):
        arrived(yfinr.at[s], YF + s)
        copy = pltpu.make_async_copy(
            yfinr.at[s],
            ig_hbm.at[:, pl.ds(pl.multiple_of((1 - xl) * HALF + s * CS, 128), CS)],
            lsem.at[2 * KC + 2 + S + s],
        )
        copy.start()
        outs.append(copy)
    for copy in started:
        copy.wait_send()
    for copy in outs:
        copy.wait()


def per_device(block_input, query_weight, query_gain, query_grad):
    hbm = pl.BlockSpec(memory_space=pl.ANY)
    vmem = pl.BlockSpec(memory_space=pltpu.VMEM)
    return pl.pallas_call(
        kernel,
        out_shape=(
            jax.ShapeDtypeStruct((T // NT, D), BF16),
            jax.ShapeDtypeStruct((80, F), F32),
        ),
        in_specs=[hbm, hbm, vmem, hbm],
        out_specs=(hbm, hbm),
        scratch_shapes=[
            pltpu.VMEM((T, D), BF16),
            pltpu.VMEM((D, T), BF16),
            pltpu.VMEM((F, D), BF16),
            pltpu.VMEM((F, HALF), BF16),
            pltpu.VMEM((F, HALF), BF16),
            pltpu.VMEM((F, T), BF16),
            pltpu.VMEM((NT, 4, 128), F32),
            pltpu.VMEM((256, T), BF16),
            pltpu.VMEM((256, T), BF16),
            pltpu.VMEM((F, T), BF16),
            pltpu.VMEM((4, 4, 240, 128), BF16),
            pltpu.VMEM((4, 4, 240, 128), BF16),
            pltpu.VMEM((4, 4, 240, 128), F32),
            pltpu.VMEM((16, 240, 128), BF16),
            pltpu.VMEM((16, 240, 128), BF16),
            pltpu.VMEM((9, 160, 128), BF16),
            pltpu.VMEM((80, F), F32),
            pltpu.VMEM((S, T, CS), F32),
            pltpu.VMEM((8, S, 32, CS), BF16),
            pltpu.VMEM((8, S, 32, CS), BF16),
            pltpu.VMEM((S, 32, CS), BF16),
            pltpu.VMEM((S, 16, CS), BF16),
            pltpu.SemaphoreType.DMA((2 * KC + 3 + 2 * S,)),
            pltpu.SemaphoreType.DMA((NSEM,)),
            pltpu.SemaphoreType.DMA((NSEM,)),
        ],
        compiler_params=pltpu.CompilerParams(
            collective_id=0, has_side_effects=True, vmem_limit_bytes=40 * 1024 * 1024
        ),
    )(block_input, query_weight, query_gain.reshape(1, F), query_grad)


def solution(mesh):
    return jax.shard_map(
        per_device,
        mesh=mesh,
        in_specs=(P("dp", None), P("tensor", None), P("tensor"), P("tensor", "dp")),
        out_specs=(P(("dp", "tensor"), None), P("dp", "tensor")),
        check_vma=False,
    )
```

time: 200 us -> 68.4 us (0.34)
  waiting for transfers between devices: 130 us -> 0 us
  Pallas kernels: 0 us -> 60.9 us
  local copies, waits for them, and re-layouts: 24 us -> 6.03 us
  blocking collectives: 15.8 us -> 0 us
  between operations: 13.8 us -> 0.65 us
  matrix products: 8.58 us -> 0 us
  starting transfers between devices: 4.56 us -> 0 us
  other arithmetic: 2.98 us -> 0 us
    reduce_scatter x3 -> x0, waiting for transfers between devices: 130 us -> none  [reduced_to_own(): tiles = lax.psum_scatter(tiles, axes[k], scatter_dimension=0, tiled=True)]
    pallas_call x0 -> x1, Pallas kernels: none -> 60.9 us  [per_device(): pl.pallas_call(kernel, out_shape=(jax.ShapeDtypeStruct((T // NT, D), BF16...]
    all_to_all x1 -> x0, blocking collectives: 15.8 us -> none  [sent_to_all(): lax.all_to_all(jnp.broadcast_to(x[None], (size, *x.shape)), axis, 0, 0, t...]
    another operation x1 -> x0, local copies, waits for them, and re-layouts: 12 us -> none  [reduced_to_own(): tiles = tiles.reshape(*(lax.axis_size(a) for a in axes), *inside)]
    transpose x1 -> x0, local copies, waits for them, and re-layouts: 10.3 us -> none  [reduced_to_own(): tiles = jnp.moveaxis(tiles, order, range(len(axes))).reshape(-1, *inside)]
    dot_general x3 -> x0, matrix products: 8.58 us -> none  [the longest x1 3.81 us: per_device(): lax.dot_general(columns, query_weight, (((0,), (0,)), ((), ())), preferre...]
    all_to_all x1 -> x0, starting transfers between devices: 4.45 us -> none  [sent_and_summed(): lax.all_to_all(tiles, axis, split_axis=0, concat_axis=0, tiled=True)]
    unnamed x6 -> x10, local copies, waits for them, and re-layouts: 1.68 us -> 6.03 us
  transfers between devices with their start and end apart: 4 -> 0, of which waited for: 3 -> 0; matrix products, arithmetic and copies ran while one was open for 3% -> 0% of each run, Pallas kernels for 0% -> 0%
where the time goes in v1:
time: 68.4 us; the launch traced here: 67.6 us
  Pallas kernels  60.9 us (89%)
  local copies, waits for them, and re-layouts  6.03 us (9%)
    pallas_call x1, Pallas kernels, per_device(): pl.pallas_call(kernel, out_shape=(jax.ShapeDtypeStruct((T // NT, D), BF16...  60.9 us
    unnamed x10, local copies, waits for them, and re-layouts  6.03 us

profile of v1, /device:TPU:1, one launch (start us, length us, event | category | flops | bytes accessed | tf_op | source)
XLA Modules:
  0.0 67.6 jit_solution(12932508520148249619)
XLA Ops:
  0.6 0.0 copy-start
  0.6 1.7 %copy-done = bf16[256,5120]{1,0:T(8,128)(2,1)S(1)} copy-done((bf16[256,5120]{1,0:T(8,128)(2,1)S(1)}, bf16[256,5120]{1,0:T(8,128)(2,1)}, u32[]{:S(2)}) %copy-start) | copy-done | bytes 2621464
  2.4 0.0 copy-start.1
  2.4 1.4 %copy-done.1 = bf16[160,5120]{1,0:T(8,128)(2,1)S(1)} copy-done((bf16[160,5120]{1,0:T(8,128)(2,1)S(1)}, bf16[160,5120]{1,0:T(8,128)(2,1)}, u32[]{:S(2)}) %copy-start.1) | copy-done | bytes 1638424
  3.8 0.0 copy-start.2
  3.8 0.9 %copy-done.2 = bf16[160,256]{1,0:T(8,128)(2,1)S(1)} copy-done((bf16[160,256]{1,0:T(8,128)(2,1)S(1)}, bf16[160,256]{1,0:T(8,128)(2,1)}, u32[]{:S(2)}) %copy-start.2) | copy-done | bytes 81944
  4.7 0.0 copy-start.3
  4.7 0.7 %copy-done.3 = f32[160]{0:T(256)S(1)} copy-done((f32[160]{0:T(256)S(1)}, f32[160]{0:T(256)}, u32[]{:S(2)}) %copy-start.3) | copy-done | bytes 664
  5.4 60.9 %shard_map.59 = (bf16[16,5120]{1,0:T(8,128)(2,1)S(1)}, f32[80,160]{1,0:T(8,128)S(1)}) custom-call(bf16[256,5120]{1,0:T(8,128)(2,1)S(1)} %copy-done, bf16[160,5120]{1,0:T(8,128)(2,1)S(1)} %copy-done.1, f32[1,160]{1,0:T(1,128)S(1)} %bitcast.1, bf16[160,256]{1,0:T(8,128)(2,1)S(1)} %copy-done.2), custom_call_target="tpu_custom_call" | custom-call | tf_op jit(solution)/shard_map/pallas_call | solution.py:315
  66.3 0.7 copy.8
  66.9 0.6 copy.9
Async XLA Ops:
  0.6 1.7 %copy-start = (bf16[256,5120]{1,0:T(8,128)(2,1)S(1)}, bf16[256,5120]{1,0:T(8,128)(2,1)}, u32[]{:S(2)}) copy-start(bf16[256,5120]{1,0:T(8,128)(2,1)} %x_hbm.1) | copy-start | bytes 7864324
  2.4 1.4 %copy-start.1 = (bf16[160,5120]{1,0:T(8,128)(2,1)S(1)}, bf16[160,5120]{1,0:T(8,128)(2,1)}, u32[]{:S(2)}) copy-start(bf16[160,5120]{1,0:T(8,128)(2,1)} %w_hbm.1) | copy-start | bytes 4915204
  3.8 0.9 %copy-start.2 = (bf16[160,256]{1,0:T(8,128)(2,1)S(1)}, bf16[160,256]{1,0:T(8,128)(2,1)}, u32[]{:S(2)}) copy-start(bf16[160,256]{1,0:T(8,128)(2,1)} %qg_hbm.1) | copy-start | bytes 245764
  4.7 0.7 %copy-start.3 = (f32[160]{0:T(256)S(1)}, f32[160]{0:T(256)}, u32[]{:S(2)}) copy-start(f32[160]{0:T(256)} %param.6) | copy-start | bytes 1924

commit v2 on v1

v2 whole, which is shorter than its diff:
```python
import jax
import jax.numpy as jnp
from jax import lax
from jax.experimental import pallas as pl
from jax.experimental.pallas import tpu as pltpu
from jax.sharding import PartitionSpec as P

MESH = pl.DeviceIdType.MESH
F32, BF16 = jnp.float32, jnp.bfloat16

NT, NY, NZ = 16, 8, 16
T, F, D = 256, 160, 5120
HALF = D // 2
S = 4
CS = HALF // S
KC = 4
KW = D // KC
HQ = F * NT
epsilon = 1e-6

PARENT = {8: 7, 7: 5, 6: 5, 5: 0, 4: 3, 3: 1, 2: 1, 1: 0, -7: -5, -6: -5, -5: 0, -4: -3, -3: -1, -2: -1, -1: 0}
CROSS = {8: 7, 7: 7, 6: 5, 5: 5, 4: 3, 3: 3, 2: 1, 1: 1, 0: 0, -7: -5, -6: -5, -5: -5, -4: -3, -3: -3, -2: -1, -1: -1}
GROUPS = ((8, 7, -7), (6, -6, 5, -5), (4, -4, 3, -3), (2, -2, 1, -1, 0))
ORDER = sum(GROUPS, ())
AT = {r: i for i, r in enumerate(ORDER)}
STAGES = ((7, 3, -3), (5, -5, 1, -1))
JOINS = STAGES[0] + STAGES[1] + (0,)
SLOT, JOIN_SLOTS = {}, {}
for j in JOINS:
    first = len(SLOT)
    for r in ORDER:
        if PARENT.get(r) == j:
            SLOT["own", r] = len(SLOT)
        if CROSS[r] == j:
            SLOT["cross", r] = len(SLOT)
    JOIN_SLOTS[j] = (first, len(SLOT) - first)
NSLOT = len(SLOT)
PACK = 112

YSTEPS = ((4, -3), (3, -2), (2, -1), (1,))
YHEADS = (4, -3)
YSLOT = {("f", 3): 0, ("f", 2): 1, ("f", 1): 2, ("f", 0): 3, ("b", -2): 4, ("b", -1): 5, ("b", 0): 6}

SUMS, WX, WD, PG = 0, 1, 3, 5
DD = 6
ZC = DD + len(GROUPS)
YC = ZC + len(JOINS)
YF = YC + 7 * S
NRECV = YF + 1
S_SUMS, S_WX, S_WD, S_PG, S_DD, S_Z, S_Y, S_YF = range(8)
L_QG, L_GAIN, L_WH, L_OUT = 2 * KC, 2 * KC + 1, 2 * KC + 2, 2 * KC + 3


def dot(a, b, dims):
    return lax.dot_general(a, b, (dims, ((), ())), preferred_element_type=F32)


def packed(v):
    rest = v[:, 128:]
    tile = rest[:16]
    for j in (1, 2, 3):
        tile = tile + pltpu.roll(rest[16 * j : 16 * j + 16], 32 * j, 1)
    return v[:, :128], tile, rest[64:]


def kernel(
    x_hbm, w_hbm, gain_hbm, qg_hbm, ig_hbm, wg_hbm,
    x_v, xt_v, w_v, wst_v, gain_v, qg_v, sums_v, pga_v, pgs_v, pgt_v,
    dsend, drecv, own_v, zx_v, zs_v, zrecv, wg_v,
    part_v, ysend, yrecv, yfin, out_v,
    lsem, ssem, rsem,
):
    d = lax.axis_index("dp")
    t = lax.axis_index("tensor")
    core = lax.rem(d, 2)
    z = lax.rem(lax.div(d, 2), NZ)
    xh = lax.div(d, 2 * NZ)
    y = lax.rem(t, NY)
    xl = lax.div(t, NY)
    sgn = 1 - 2 * core

    def dev(xh_, z_, core_, xl_, y_):
        return {"dp": (xh_ * NZ + z_) * 2 + core_, "tensor": xl_ * NY + y_}

    def zat(r):
        return lax.rem(z + sgn * r + 2 * NZ, NZ)

    def yat(r):
        return lax.rem(y + sgn * r + 2 * NY, NY)

    sibling = dev(xh, z, 1 - core, xl, y)
    partner = dev(xh, z, core, 1 - xl, y)
    across = dev(1 - xh, z, core, 1 - xl, y)

    loads = []
    for k in range(KC):
        cols = pl.ds(k * KW, KW)
        loads.append((
            pltpu.make_async_copy(x_hbm.at[:, cols], x_v.at[:, cols], lsem.at[k]),
            pltpu.make_async_copy(w_hbm.at[:, cols], w_v.at[:, cols], lsem.at[KC + k]),
        ))
    for a, b in loads:
        a.start()
        b.start()
    qg_load = pltpu.make_async_copy(qg_hbm, qg_v, lsem.at[L_QG])
    qg_load.start()
    gain_load = pltpu.make_async_copy(gain_hbm, gain_v, lsem.at[L_GAIN])
    gain_load.start()
    myhalf = pl.ds(pl.multiple_of(xl * HALF, 128), HALF)
    otherhalf = pl.ds(pl.multiple_of((1 - xl) * HALF, 128), HALF)
    wh_load = pltpu.make_async_copy(w_hbm.at[:, myhalf], wst_v.at[:F], lsem.at[L_WH])
    wh_load.start()

    barrier = pltpu.get_barrier_semaphore()
    peers = [{"dp": d, "tensor": lax.rem(t + o, NT)} for o in range(1, NT)]
    peers += [across, sibling]
    peers += [dev(xh, zat(r), core, xl, y) for r in (1, -1, 2, -2, 5, -5)]
    peers += [dev(1 - xh, zat(r), core, xl, y) for r in (0, 1, -1, 2, -2)]
    for p in peers:
        pl.semaphore_signal(barrier, inc=1, device_id=p, device_id_type=MESH)

    pt = None
    for k, (a, b) in enumerate(loads):
        a.wait()
        b.wait()
        cols = slice(k * KW, (k + 1) * KW)
        term = dot(w_v[:, cols], x_v[:, cols], ((1,), (1,)))
        pt = term if pt is None else pt + term
    qg_load.wait()
    gain_load.wait()
    rows = lax.broadcasted_iota(jnp.int32, (F, F), 0)
    lanes = lax.broadcasted_iota(jnp.int32, (F, F), 1)
    gain = jnp.sum(jnp.where(rows == lanes, gain_v[...], 0.0), axis=1, keepdims=True)
    sg = qg_v[...].astype(F32) * gain
    sq = jnp.sum(pt * pt, axis=0, keepdims=True)
    cr = jnp.sum(sg * pt, axis=0, keepdims=True)
    sums_v[t, 0:1, :] = sq[:, :128]
    sums_v[t, 1:2, :] = sq[:, 128:]
    sums_v[t, 2:3, :] = cr[:, :128]
    sums_v[t, 3:4, :] = cr[:, 128:]

    pl.semaphore_wait(barrier, len(peers))

    def send(src, dst, ssem_at, rsem_at, device):
        pltpu.make_async_remote_copy(
            src_ref=src, dst_ref=dst, send_sem=ssem.at[ssem_at], recv_sem=rsem.at[rsem_at],
            device_id=device, device_id_type=MESH,
        ).start()

    def handle(ref, ssem_at, rsem_at):
        return pltpu.make_async_remote_copy(
            src_ref=ref, dst_ref=ref, send_sem=ssem.at[ssem_at], recv_sem=rsem.at[rsem_at],
            device_id=sibling, device_id_type=MESH,
        )

    def arrived(ref, rsem_at):
        handle(ref, 0, rsem_at).wait_recv()

    def left(ref, ssem_at):
        handle(ref, ssem_at, 0).wait_send()

    for p in peers[: NT - 1]:
        send(sums_v.at[t], sums_v.at[t], S_SUMS, SUMS, p)

    wpart = wst_v.at[F:]
    for n, who in enumerate((partner, across)):
        src = pl.ds(pl.multiple_of((1 - xl) * HALF + (2 * n + core) * CS, 128), CS)
        dst = pl.ds(pl.multiple_of((2 * n + core) * CS, 128), CS)
        send(w_v.at[:, src], wpart.at[:, dst], S_WX, WX + n, who)

    for k in range(D // 256):
        turned = x_v[:, k * 256 : (k + 1) * 256].T
        at, end = k * 256, (k + 1) * 256
        while at < end:
            h, zz, o = at // HALF, at % HALF // 160, at % 160
            n = min(160 - o, end - at)
            xt_v[zz, h * 160 + o : h * 160 + o + n, :] = turned[at - k * 256 : at - k * 256 + n]
            at += n
    pga_v[F:, :] = jnp.zeros((256 - F, T), BF16)

    arrived(sums_v.at[: NT - 1], SUMS)
    total = sums_v[0]
    for s in range(1, NT):
        total = total + sums_v[s]
    sq = jnp.concatenate([total[0:1], total[1:2]], axis=1)
    cr = jnp.concatenate([total[2:3], total[3:4]], axis=1)
    inv = 1.0 / jnp.sqrt(sq / HQ + epsilon)
    coef = inv * inv * inv * (cr / HQ)
    pg = (inv * sg - coef * pt).astype(BF16)
    pga_v[:F, :] = pg
    pgs_v[:F, :] = pg
    send(pga_v.at[:F], pgs_v.at[F:], S_PG, PG, partner)

    def blocks(g):
        for r in GROUPS[g]:
            v = dot(xt_v[zat(r)], pga_v[...], ((1,), (1,)))
            mirror = r if r in (0, 8) else -r
            for h in (0, 1):
                a, b = v[h * 160 : h * 160 + 80], v[h * 160 + 80 : h * 160 + 160]
                mine = packed(jnp.where(core == 0, a, b))
                other = packed(jnp.where(core == 0, b, a))
                for ref, i, parts in ((own_v, AT[r], mine), (dsend, AT[mirror], other)):
                    ref[i, h, :80, :] = parts[0].astype(ref.dtype)
                    ref[i, h, 80:96, :] = parts[1].astype(ref.dtype)
                    ref[i, h, 96:, :] = parts[2].astype(ref.dtype)
        at = pl.ds(AT[GROUPS[g][0]], len(GROUPS[g]))
        send(dsend.at[at], drecv.at[at], S_DD, DD + g, sibling)

    def local(r, h):
        return own_v[AT[r], h] + drecv[AT[r], h].astype(F32)

    def zsend(r, v):
        i, slot = AT[r], SLOT["own", r]
        zs_v[i] = v.astype(BF16)
        send(
            zs_v.at[i], zrecv.at[slot], S_Z, ZC + JOINS.index(PARENT[r]),
            dev(xh, zat(r - PARENT[r]), core, xl, y),
        )

    def zleaf(g):
        at = pl.ds(AT[GROUPS[g][0]], len(GROUPS[g]))
        arrived(drecv.at[at], DD + g)
        for r in GROUPS[g]:
            i, slot = AT[r], SLOT["cross", r]
            zx_v[i] = local(r, 1 - xh).astype(BF16)
            send(
                zx_v.at[i], zrecv.at[slot], S_Z, ZC + JOINS.index(CROSS[r]),
                dev(1 - xh, zat(r - CROSS[r]), core, xl, y),
            )
            if r not in JOINS:
                zsend(r, local(r, xh))

    def joined(r):
        first, n = JOIN_SLOTS[r]
        arrived(zrecv.at[pl.ds(first, n)], ZC + JOINS.index(r))
        v = local(r, xh)
        for k in range(first, first + n):
            v = v + zrecv[k].astype(F32)
        return v

    def zstage(k):
        for r in STAGES[k]:
            zsend(r, joined(r))

    def yrows(r):
        return pl.multiple_of(yat(r) * 16, 16)

    def ystep(k, s):
        for r in YSTEPS[k]:
            side, nxt = ("f", r - 1) if r > 0 else ("b", r + 1)
            at = yrows(r)
            new = [part_v[s, pl.ds(at + h * 128, 16), :] for h in (0, 1)]
            if r not in YHEADS:
                slot = YSLOT[side, r]
                arrived(yrecv.at[slot, s], YC + slot * S + s)
                new = [v + yrecv[slot, s, h * 16 : h * 16 + 16, :].astype(F32) for h, v in enumerate(new)]
            slot = YSLOT[side, nxt]
            for h, v in enumerate(new):
                ysend[slot, s, h * 16 : h * 16 + 16, :] = v.astype(BF16)
            send(
                ysend.at[slot, s], yrecv.at[slot, s], S_Y, YC + slot * S + s,
                dev(xh, z, core, xl, yat(1 if r > 0 else -1)),
            )

    blocks(0)
    blocks(1)
    zleaf(0)
    blocks(2)
    zleaf(1)
    blocks(3)
    zleaf(2)
    zleaf(3)

    for n in (0, 1):
        cols = pl.ds(pl.multiple_of((2 * n + core) * CS, 128), CS)
        arrived(wpart.at[:, cols], WX + n)
        send(wpart.at[:, cols], wpart.at[:, cols], S_WD, WD + n, sibling)
    wh_load.wait()
    arrived(pgs_v.at[F:], PG)
    pgt_v[...] = pgs_v[...].T
    for n in (0, 1):
        cols = pl.ds(pl.multiple_of((2 * n + 1 - core) * CS, 128), CS)
        arrived(wpart.at[:, cols], WD + n)
    for s in range(S):
        part_v[s] = dot(pgt_v[...], wst_v[:, s * CS : (s + 1) * CS], ((1,), (0,)))
        ystep(0, s)

    zstage(0)
    for s in range(S):
        ystep(1, s)
    zstage(1)
    for s in range(S):
        ystep(2, s)
    for s in range(S):
        ystep(3, s)

    for s in range(S):
        slots = (YSLOT["f", 0], YSLOT["b", 0])
        for slot in slots:
            arrived(yrecv.at[slot, s], YC + slot * S + s)
        for h in (0, 1):
            rows = slice(h * 16, h * 16 + 16)
            v = part_v[s, pl.ds(yrows(0) + h * 128, 16), :]
            for slot in slots:
                v = v + yrecv[slot, s, rows, :].astype(F32)
            yfin[s, rows, :] = v.astype(BF16)
        cols = pl.ds(pl.multiple_of(xl * HALF + s * CS, 128), CS)
        send(yfin.at[s, pl.ds(pl.multiple_of((1 - xl) * 16, 16), 16)], out_v.at[:, cols], S_YF, YF, partner)
        out_v[:, cols] = yfin[s, pl.ds(pl.multiple_of(xl * 16, 16), 16), :]
    outs = [pltpu.make_async_copy(out_v.at[:, myhalf], ig_hbm.at[:, myhalf], lsem.at[L_OUT])]
    outs[0].start()

    v = joined(0)
    wg_v[:, :128] = v[:80]
    wg_v[:16, 128:] = v[80:96, :32]
    for j in (1, 2, 3):
        wg_v[16 * j : 16 * j + 16, 128:] = pltpu.roll(v[80:96], 128 - 32 * j, 1)[:, :32]
    wg_v[64:, 128:] = v[96:, :32]
    outs.append(pltpu.make_async_copy(wg_v, wg_hbm, lsem.at[L_OUT + 1]))
    outs[1].start()

    arrived(out_v.at[:, otherhalf], YF)
    outs.append(pltpu.make_async_copy(out_v.at[:, otherhalf], ig_hbm.at[:, otherhalf], lsem.at[L_OUT + 2]))
    outs[2].start()
    left(sums_v.at[: NT - 1], S_SUMS)
    left(wpart.at[:, : 2 * CS], S_WX)
    left(wpart.at[:, : 2 * CS], S_WD)
    left(pgs_v.at[F:], S_PG)
    left(dsend, S_DD)
    left(zrecv, S_Z)
    left(yrecv, S_Y)
    left(out_v.at[:, otherhalf], S_YF)
    for copy in outs:
        copy.wait()


def per_device(block_input, query_weight, query_gain, query_grad):
    hbm = pl.BlockSpec(memory_space=pltpu.HBM)
    anywhere = pl.BlockSpec(memory_space=pl.ANY)
    return pl.pallas_call(
        kernel,
        out_shape=(
            jax.ShapeDtypeStruct((T // NT, D), BF16),
            jax.ShapeDtypeStruct((80, F), F32),
        ),
        in_specs=[hbm, hbm, hbm, hbm],
        out_specs=(anywhere, anywhere),
        scratch_shapes=[
            pltpu.VMEM((T, D), BF16),
            pltpu.VMEM((NZ, 320, T), BF16),
            pltpu.VMEM((F, D), BF16),
            pltpu.VMEM((2 * F, HALF), BF16),
            pltpu.VMEM((1, F), F32),
            pltpu.VMEM((F, T), BF16),
            pltpu.VMEM((NT, 4, 128), F32),
            pltpu.VMEM((256, T), BF16),
            pltpu.VMEM((2 * F, T), BF16),
            pltpu.VMEM((T, 2 * F), BF16),
            pltpu.VMEM((16, 2, PACK, 128), BF16),
            pltpu.VMEM((16, 2, PACK, 128), BF16),
            pltpu.VMEM((16, 2, PACK, 128), F32),
            pltpu.VMEM((16, PACK, 128), BF16),
            pltpu.VMEM((16, PACK, 128), BF16),
            pltpu.VMEM((NSLOT, PACK, 128), BF16),
            pltpu.VMEM((80, F), F32),
            pltpu.VMEM((S, T, CS), F32),
            pltpu.VMEM((7, S, 32, CS), BF16),
            pltpu.VMEM((7, S, 32, CS), BF16),
            pltpu.VMEM((S, 32, CS), BF16),
            pltpu.VMEM((T // NT, D), BF16),
            pltpu.SemaphoreType.DMA((L_OUT + 3,)),
            pltpu.SemaphoreType.DMA((8,)),
            pltpu.SemaphoreType.DMA((NRECV,)),
        ],
        compiler_params=pltpu.CompilerParams(
            collective_id=0, has_side_effects=True, vmem_limit_bytes=40 * 1024 * 1024
        ),
    )(*(pltpu.with_memory_space_constraint(a, pltpu.HBM) for a in (block_input, query_weight, query_gain.reshape(1, F), query_grad)))


def solution(mesh):
    return jax.shard_map(
        per_device,
        mesh=mesh,
        in_specs=(P("dp", None), P("tensor", None), P("tensor"), P("tensor", "dp")),
        out_specs=(P(("dp", "tensor"), None), P("dp", "tensor")),
        check_vma=False,
    )
```

time: 68.4 us -> 59.4 us (0.87)
  the two profiles are of different devices: /device:TPU:1 before, /device:TPU:2 now
where the time goes in v2:
time: 59.4 us; the launch traced here: 59.3 us
  Pallas kernels  57.3 us (96%)
  local copies, waits for them, and re-layouts  1.3 us (2%)
  between operations  0.64 us (1%)
    pallas_call x1, Pallas kernels, per_device(): pl.pallas_call(kernel, out_shape=(jax.ShapeDtypeStruct((T // NT, D), BF16...  57.3 us
    unnamed x2, local copies, waits for them, and re-layouts  1.3 us

profile of v2, /device:TPU:2, one launch (start us, length us, event | category | flops | bytes accessed | tf_op | source)
XLA Modules:
  0.0 59.3 jit_solution(4459230357320650954)
XLA Ops:
  0.6 57.3 %shard_map.59 = (bf16[16,5120]{1,0:T(8,128)(2,1)S(1)}, f32[80,160]{1,0:T(8,128)S(1)}) custom-call(bf16[256,5120]{1,0:T(8,128)(2,1)} %x_hbm.1, bf16[160,5120]{1,0:T(8,128)(2,1)} %w_hbm.1, f32[1,160]{1,0:T(1,128)} %bitcast.1, bf16[160,256]{1,0:T(8,128)(2,1)} %qg_hbm.1), custom_call_target="tpu_custom_call" | custom-call | tf_op jit(solution)/shard_map/pallas_call | solution.py:340
  58.0 0.7 %copy.8 = bf16[16,5120]{1,0:T(8,128)(2,1)} copy(bf16[16,5120]{1,0:T(8,128)(2,1)S(1)} %get-tuple-element.4) | data formatting | bytes 327680
  58.6 0.6 %copy.9 = f32[80,160]{1,0:T(8,128)} copy(f32[80,160]{1,0:T(8,128)S(1)} %get-tuple-element.5) | data formatting | bytes 102400

commit v3 on v2

--- a/solution.py
+++ b/solution.py
@@ -19,22 +19,24 @@
 epsilon = 1e-6
 
 PARENT = {8: 7, 7: 5, 6: 5, 5: 0, 4: 3, 3: 1, 2: 1, 1: 0, -7: -5, -6: -5, -5: 0, -4: -3, -3: -1, -2: -1, -1: 0}
-CROSS = {8: 7, 7: 7, 6: 5, 5: 5, 4: 3, 3: 3, 2: 1, 1: 1, 0: 0, -7: -5, -6: -5, -5: -5, -4: -3, -3: -3, -2: -1, -1: -1}
+CROSS = {8: 7, 7: 7, 6: 5, 5: 5, -7: -5, -6: -5, -5: -5, 1: 0, -1: 0, 0: 0}
 GROUPS = ((8, 7, -7), (6, -6, 5, -5), (4, -4, 3, -3), (2, -2, 1, -1, 0))
 ORDER = sum(GROUPS, ())
 AT = {r: i for i, r in enumerate(ORDER)}
-STAGES = ((7, 3, -3), (5, -5, 1, -1))
-JOINS = STAGES[0] + STAGES[1] + (0,)
+JOINS = (7, 5, -5, 3, -3, 1, -1, 0)
 SLOT, JOIN_SLOTS = {}, {}
+count = 0
 for j in JOINS:
-    first = len(SLOT)
+    first = count
     for r in ORDER:
         if PARENT.get(r) == j:
-            SLOT["own", r] = len(SLOT)
-        if CROSS[r] == j:
-            SLOT["cross", r] = len(SLOT)
-    JOIN_SLOTS[j] = (first, len(SLOT) - first)
-NSLOT = len(SLOT)
+            SLOT["own", r] = count
+            count += 2 if abs(r) < 5 and j else 1
+        if CROSS.get(r) == j:
+            SLOT["cross", r] = count
+            count += 1
+    JOIN_SLOTS[j] = (first, count - first)
+NSLOT = count
 PACK = 112
 
 YSTEPS = ((4, -3), (3, -2), (2, -1), (1,))
@@ -65,8 +67,8 @@
 
 def kernel(
     x_hbm, w_hbm, gain_hbm, qg_hbm, ig_hbm, wg_hbm,
-    x_v, xt_v, w_v, wst_v, gain_v, qg_v, sums_v, pga_v, pgs_v, pgt_v,
-    dsend, drecv, own_v, zx_v, zs_v, zrecv, wg_v,
+    x_v, xt_v, w_v, wst_v, gain_v, qg_v, sums_v, pga_v, pgp_v, sgt_v, ptt_v,
+    dsend, drecv, own_v, zs_v, zrecv, wg_v,
     part_v, ysend, yrecv, yfin, out_v,
     lsem, ssem, rsem,
 ):
@@ -177,6 +179,8 @@
             xt_v[zz, h * 160 + o : h * 160 + o + n, :] = turned[at - k * 256 : at - k * 256 + n]
             at += n
     pga_v[F:, :] = jnp.zeros((256 - F, T), BF16)
+    sgt_v[...] = sg.T
+    ptt_v[...] = pt.T
 
     arrived(sums_v.at[: NT - 1], SUMS)
     total = sums_v[0]
@@ -188,8 +192,7 @@
     coef = inv * inv * inv * (cr / HQ)
     pg = (inv * sg - coef * pt).astype(BF16)
     pga_v[:F, :] = pg
-    pgs_v[:F, :] = pg
-    send(pga_v.at[:F], pgs_v.at[F:], S_PG, PG, partner)
+    send(pga_v.at[:F], pgp_v, S_PG, PG, partner)
 
     def blocks(g):
         for r in GROUPS[g]:
@@ -209,11 +212,25 @@
     def local(r, h):
         return own_v[AT[r], h] + drecv[AT[r], h].astype(F32)
 
-    def zsend(r, v):
-        i, slot = AT[r], SLOT["own", r]
-        zs_v[i] = v.astype(BF16)
+    def zcross(r, v):
+        zs_v[AT[r], 1 - xh] = v.astype(BF16)
         send(
-            zs_v.at[i], zrecv.at[slot], S_Z, ZC + JOINS.index(PARENT[r]),
+            zs_v.at[AT[r], 1 - xh], zrecv.at[SLOT["cross", r]], S_Z, ZC + JOINS.index(CROSS[r]),
+            dev(1 - xh, zat(r - CROSS[r]), core, xl, y),
+        )
+
+    def zown(r, v):
+        zs_v[AT[r], xh] = v.astype(BF16)
+        send(
+            zs_v.at[AT[r], xh], zrecv.at[SLOT["own", r]], S_Z, ZC + JOINS.index(PARENT[r]),
+            dev(xh, zat(r - PARENT[r]), core, xl, y),
+        )
+
+    def zboth(r, pair):
+        for h, v in enumerate(pair):
+            zs_v[AT[r], h] = v.astype(BF16)
+        send(
+            zs_v.at[AT[r]], zrecv.at[pl.ds(SLOT["own", r], 2)], S_Z, ZC + JOINS.index(PARENT[r]),
             dev(xh, zat(r - PARENT[r]), core, xl, y),
         )
 
@@ -221,26 +238,40 @@
         at = pl.ds(AT[GROUPS[g][0]], len(GROUPS[g]))
         arrived(drecv.at[at], DD + g)
         for r in GROUPS[g]:
-            i, slot = AT[r], SLOT["cross", r]
-            zx_v[i] = local(r, 1 - xh).astype(BF16)
-            send(
-                zx_v.at[i], zrecv.at[slot], S_Z, ZC + JOINS.index(CROSS[r]),
-                dev(1 - xh, zat(r - CROSS[r]), core, xl, y),
-            )
+            if abs(r) >= 5 or r == 0:
+                zcross(r, local(r, 1 - xh))
             if r not in JOINS:
-                zsend(r, local(r, xh))
+                if abs(r) >= 5:
+                    zown(r, local(r, xh))
+                else:
+                    zboth(r, [local(r, h) for h in (0, 1)])
 
     def joined(r):
         first, n = JOIN_SLOTS[r]
         arrived(zrecv.at[pl.ds(first, n)], ZC + JOINS.index(r))
-        v = local(r, xh)
-        for k in range(first, first + n):
-            v = v + zrecv[k].astype(F32)
-        return v
-
-    def zstage(k):
-        for r in STAGES[k]:
-            zsend(r, joined(r))
+        slots = range(first, first + n)
+        if abs(r) >= 5 or r == 0:
+            v = local(r, xh)
+            for k in slots:
+                v = v + zrecv[k].astype(F32)
+            return v
+        pair = []
+        for h in ((0, 1) if abs(r) == 3 else (xh, 1 - xh)):
+            v = local(r, h)
+            for k in range(first, first + n, 2):
+                v = v + zrecv[k + h].astype(F32)
+            pair.append(v)
+        return pair
+
+    def zjoin(r):
+        v = joined(r)
+        if abs(r) == 5 or r == 7:
+            zown(r, v)
+        elif abs(r) == 3:
+            zboth(r, v)
+        else:
+            zcross(r, v[1])
+            zown(r, v[0])
 
     def yrows(r):
         return pl.multiple_of(yat(r) * 16, 16)
@@ -264,33 +295,41 @@
 
     blocks(0)
     blocks(1)
+    for n in (0, 1):
+        cols = pl.ds(pl.multiple_of((2 * n + core) * CS, 128), CS)
+        arrived(wpart.at[:, cols], WX + n)
+        send(wpart.at[:, cols], wpart.at[:, cols], S_WD, WD + n, sibling)
+    wh_load.wait()
+    both = jnp.concatenate([inv, coef], axis=0)
+    both = jnp.concatenate([both, jnp.zeros((6, T), F32)], axis=0).T
+    own = (both[:, 0:1] * sgt_v[...] - both[:, 1:2] * ptt_v[...]).astype(BF16)
+    for s in range(S):
+        part_v[s] = dot(own, wst_v[:F, s * CS : (s + 1) * CS], ((1,), (0,)))
     zleaf(0)
+    arrived(pgp_v, PG)
+    theirs = pgp_v[...].T
+    for n in (0, 1):
+        cols = pl.ds(pl.multiple_of((2 * n + 1 - core) * CS, 128), CS)
+        arrived(wpart.at[:, cols], WD + n)
+    for s in range(S):
+        part_v[s] += dot(theirs, wst_v[F:, s * CS : (s + 1) * CS], ((1,), (0,)))
+        ystep(0, s)
     blocks(2)
     zleaf(1)
     blocks(3)
     zleaf(2)
     zleaf(3)
-
-    for n in (0, 1):
-        cols = pl.ds(pl.multiple_of((2 * n + core) * CS, 128), CS)
-        arrived(wpart.at[:, cols], WX + n)
-        send(wpart.at[:, cols], wpart.at[:, cols], S_WD, WD + n, sibling)
-    wh_load.wait()
-    arrived(pgs_v.at[F:], PG)
-    pgt_v[...] = pgs_v[...].T
-    for n in (0, 1):
-        cols = pl.ds(pl.multiple_of((2 * n + 1 - core) * CS, 128), CS)
-        arrived(wpart.at[:, cols], WD + n)
-    for s in range(S):
-        part_v[s] = dot(pgt_v[...], wst_v[:, s * CS : (s + 1) * CS], ((1,), (0,)))
-        ystep(0, s)
-
-    zstage(0)
+    zjoin(7)
+    zjoin(-5)
     for s in range(S):
         ystep(1, s)
-    zstage(1)
+    zjoin(3)
+    zjoin(-3)
+    zjoin(5)
     for s in range(S):
         ystep(2, s)
+    zjoin(1)
+    zjoin(-1)
     for s in range(S):
         ystep(3, s)
 
@@ -325,7 +364,7 @@
     left(sums_v.at[: NT - 1], S_SUMS)
     left(wpart.at[:, : 2 * CS], S_WX)
     left(wpart.at[:, : 2 * CS], S_WD)
-    left(pgs_v.at[F:], S_PG)
+    left(pgp_v, S_PG)
     left(dsend, S_DD)
     left(zrecv, S_Z)
     left(yrecv, S_Y)
@@ -354,13 +393,13 @@
             pltpu.VMEM((F, T), BF16),
             pltpu.VMEM((NT, 4, 128), F32),
             pltpu.VMEM((256, T), BF16),
-            pltpu.VMEM((2 * F, T), BF16),
-            pltpu.VMEM((T, 2 * F), BF16),
+            pltpu.VMEM((F, T), BF16),
+            pltpu.VMEM((T, F), F32),
+            pltpu.VMEM((T, F), F32),
             pltpu.VMEM((16, 2, PACK, 128), BF16),
             pltpu.VMEM((16, 2, PACK, 128), BF16),
             pltpu.VMEM((16, 2, PACK, 128), F32),
-            pltpu.VMEM((16, PACK, 128), BF16),
-            pltpu.VMEM((16, PACK, 128), BF16),
+            pltpu.VMEM((16, 2, PACK, 128), BF16),
             pltpu.VMEM((NSLOT, PACK, 128), BF16),
             pltpu.VMEM((80, F), F32),
             pltpu.VMEM((S, T, CS), F32),

time: 59.4 us -> 55.6 us (0.936)
  the two profiles are of different devices: /device:TPU:2 before, /device:TPU:4 now
where the time goes in v3:
time: 55.6 us; the launch traced here: 55.4 us
  Pallas kernels  53.5 us (96%)
  local copies, waits for them, and re-layouts  1.3 us (2%)
  between operations  0.64 us (1%)
    pallas_call x1, Pallas kernels, per_device(): pl.pallas_call(kernel, out_shape=(jax.ShapeDtypeStruct((T // NT, D), BF16...  53.5 us
    unnamed x2, local copies, waits for them, and re-layouts  1.3 us

profile of v3, /device:TPU:4, one launch (start us, length us, event | category | flops | bytes accessed | tf_op | source)
XLA Modules:
  0.0 55.4 jit_solution(4865819432133419151)
XLA Ops:
  0.6 53.5 %shard_map.59 = (bf16[16,5120]{1,0:T(8,128)(2,1)S(1)}, f32[80,160]{1,0:T(8,128)S(1)}) custom-call(bf16[256,5120]{1,0:T(8,128)(2,1)} %x_hbm.1, bf16[160,5120]{1,0:T(8,128)(2,1)} %w_hbm.1, f32[1,160]{1,0:T(1,128)} %bitcast.1, bf16[160,256]{1,0:T(8,128)(2,1)} %qg_hbm.1), custom_call_target="tpu_custom_call" | custom-call | tf_op jit(solution)/shard_map/pallas_call | solution.py:379
  54.1 0.7 %copy.8 = bf16[16,5120]{1,0:T(8,128)(2,1)} copy(bf16[16,5120]{1,0:T(8,128)(2,1)S(1)} %get-tuple-element.4) | data formatting | bytes 327680
  54.8 0.6 %copy.9 = f32[80,160]{1,0:T(8,128)} copy(f32[80,160]{1,0:T(8,128)S(1)} %get-tuple-element.5) | data formatting | bytes 102400

commit v4 on v3

--- a/solution.py
+++ b/solution.py
@@ -41,14 +41,14 @@
 
 YSTEPS = ((4, -3), (3, -2), (2, -1), (1,))
 YHEADS = (4, -3)
-YSLOT = {("f", 3): 0, ("f", 2): 1, ("f", 1): 2, ("f", 0): 3, ("b", -2): 4, ("b", -1): 5, ("b", 0): 6}
+YSLOT = {3: 0, 2: 1, 1: 2, -2: 3, -1: 4}
 
 SUMS, WX, WD, PG = 0, 1, 3, 5
 DD = 6
 ZC = DD + len(GROUPS)
 YC = ZC + len(JOINS)
-YF = YC + 7 * S
-NRECV = YF + 1
+YF = YC + 5 * S
+NRECV = YF + S
 S_SUMS, S_WX, S_WD, S_PG, S_DD, S_Z, S_Y, S_YF = range(8)
 L_QG, L_GAIN, L_WH, L_OUT = 2 * KC, 2 * KC + 1, 2 * KC + 2, 2 * KC + 3
 
@@ -69,7 +69,7 @@
     x_hbm, w_hbm, gain_hbm, qg_hbm, ig_hbm, wg_hbm,
     x_v, xt_v, w_v, wst_v, gain_v, qg_v, sums_v, pga_v, pgp_v, sgt_v, ptt_v,
     dsend, drecv, own_v, zs_v, zrecv, wg_v,
-    part_v, ysend, yrecv, yfin, out_v,
+    part_v, ysend, yrecv, ylast, yfin, out_v,
     lsem, ssem, rsem,
 ):
     d = lax.axis_index("dp")
@@ -109,7 +109,6 @@
     gain_load = pltpu.make_async_copy(gain_hbm, gain_v, lsem.at[L_GAIN])
     gain_load.start()
     myhalf = pl.ds(pl.multiple_of(xl * HALF, 128), HALF)
-    otherhalf = pl.ds(pl.multiple_of((1 - xl) * HALF, 128), HALF)
     wh_load = pltpu.make_async_copy(w_hbm.at[:, myhalf], wst_v.at[:F], lsem.at[L_WH])
     wh_load.start()
 
@@ -276,22 +275,40 @@
     def yrows(r):
         return pl.multiple_of(yat(r) * 16, 16)
 
+    def mine(r, s, h):
+        return part_v[s, pl.ds(yrows(r) + h * 128, 16), :]
+
+    def ylast_send(slot, s, rows, dest):
+        for i, who in enumerate((xl, 1 - xl)):
+            if dest is None and i == 0:
+                continue
+            src = rows.at[pl.ds(pl.multiple_of(who * 16, 16), 16)]
+            send(src, yfin.at[s, slot + i], S_YF, YF + s, dev(xh, z, core, who, y if dest is None else dest))
+
     def ystep(k, s):
         for r in YSTEPS[k]:
-            side, nxt = ("f", r - 1) if r > 0 else ("b", r + 1)
-            at = yrows(r)
-            new = [part_v[s, pl.ds(at + h * 128, 16), :] for h in (0, 1)]
+            new = [mine(r, s, h) for h in (0, 1)]
             if r not in YHEADS:
-                slot = YSLOT[side, r]
+                slot = YSLOT[r]
                 arrived(yrecv.at[slot, s], YC + slot * S + s)
                 new = [v + yrecv[slot, s, h * 16 : h * 16 + 16, :].astype(F32) for h, v in enumerate(new)]
-            slot = YSLOT[side, nxt]
+            to = yat(1 if r > 0 else -1)
+            if abs(r) == 1:
+                rows = ylast.at[0 if r > 0 else 1, s]
+            else:
+                slot = YSLOT[r - 1 if r > 0 else r + 1]
+                rows = ysend.at[slot, s]
             for h, v in enumerate(new):
-                ysend[slot, s, h * 16 : h * 16 + 16, :] = v.astype(BF16)
-            send(
-                ysend.at[slot, s], yrecv.at[slot, s], S_Y, YC + slot * S + s,
-                dev(xh, z, core, xl, yat(1 if r > 0 else -1)),
-            )
+                rows[h * 16 : h * 16 + 16, :] = v.astype(BF16)
+            if abs(r) == 1:
+                ylast_send(0 if r > 0 else 2, s, rows, to)
+            else:
+                send(rows, yrecv.at[slot, s], S_Y, YC + slot * S + s, dev(xh, z, core, xl, to))
+
+    def yown_cross(s):
+        for h in (0, 1):
+            ylast[2, s, h * 16 : h * 16 + 16, :] = mine(0, s, h).astype(BF16)
+        ylast_send(3, s, ylast.at[2, s], None)
 
     blocks(0)
     blocks(1)
@@ -306,6 +323,8 @@
     for s in range(S):
         part_v[s] = dot(own, wst_v[:F, s * CS : (s + 1) * CS], ((1,), (0,)))
     zleaf(0)
+    zleaf(1)
+    blocks(2)
     arrived(pgp_v, PG)
     theirs = pgp_v[...].T
     for n in (0, 1):
@@ -314,40 +333,34 @@
     for s in range(S):
         part_v[s] += dot(theirs, wst_v[F:, s * CS : (s + 1) * CS], ((1,), (0,)))
         ystep(0, s)
-    blocks(2)
-    zleaf(1)
+    for s in range(S):
+        yown_cross(s)
+    zleaf(2)
     blocks(3)
-    zleaf(2)
     zleaf(3)
     zjoin(7)
-    zjoin(-5)
     for s in range(S):
         ystep(1, s)
     zjoin(3)
     zjoin(-3)
+    zjoin(-5)
     zjoin(5)
     for s in range(S):
         ystep(2, s)
+    for s in range(S):
+        ystep(3, s)
     zjoin(1)
     zjoin(-1)
-    for s in range(S):
-        ystep(3, s)
-
-    for s in range(S):
-        slots = (YSLOT["f", 0], YSLOT["b", 0])
-        for slot in slots:
-            arrived(yrecv.at[slot, s], YC + slot * S + s)
-        for h in (0, 1):
-            rows = slice(h * 16, h * 16 + 16)
-            v = part_v[s, pl.ds(yrows(0) + h * 128, 16), :]
+    outs = []
+    for s in range(S):
+        arrived(yfin.at[s], YF + s)
+        own = part_v[s, pl.ds(yrows(0) + xl * 128, 16), :]
+        for who, v, slots in ((xl, own, (0, 2)), (1 - xl, 0.0, (1, 3, 4))):
             for slot in slots:
-                v = v + yrecv[slot, s, rows, :].astype(F32)
-            yfin[s, rows, :] = v.astype(BF16)
-        cols = pl.ds(pl.multiple_of(xl * HALF + s * CS, 128), CS)
-        send(yfin.at[s, pl.ds(pl.multiple_of((1 - xl) * 16, 16), 16)], out_v.at[:, cols], S_YF, YF, partner)
-        out_v[:, cols] = yfin[s, pl.ds(pl.multiple_of(xl * 16, 16), 16), :]
-    outs = [pltpu.make_async_copy(out_v.at[:, myhalf], ig_hbm.at[:, myhalf], lsem.at[L_OUT])]
-    outs[0].start()
+                v = v + yfin[s, slot].astype(F32)
+            cols = pl.ds(pl.multiple_of(who * HALF + s * CS, 128), CS)
+            out_v[:, cols] = v.astype(BF16)
+            pltpu.make_async_copy(out_v.at[:, cols], ig_hbm.at[:, cols], lsem.at[L_OUT]).start()
 
     v = joined(0)
     wg_v[:, :128] = v[:80]
@@ -356,11 +369,8 @@
         wg_v[16 * j : 16 * j + 16, 128:] = pltpu.roll(v[80:96], 128 - 32 * j, 1)[:, :32]
     wg_v[64:, 128:] = v[96:, :32]
     outs.append(pltpu.make_async_copy(wg_v, wg_hbm, lsem.at[L_OUT + 1]))
-    outs[1].start()
-
-    arrived(out_v.at[:, otherhalf], YF)
-    outs.append(pltpu.make_async_copy(out_v.at[:, otherhalf], ig_hbm.at[:, otherhalf], lsem.at[L_OUT + 2]))
-    outs[2].start()
+    outs[0].start()
+
     left(sums_v.at[: NT - 1], S_SUMS)
     left(wpart.at[:, : 2 * CS], S_WX)
     left(wpart.at[:, : 2 * CS], S_WD)
@@ -368,7 +378,8 @@
     left(dsend, S_DD)
     left(zrecv, S_Z)
     left(yrecv, S_Y)
-    left(out_v.at[:, otherhalf], S_YF)
+    left(yfin, S_YF)
+    outs.append(pltpu.make_async_copy(out_v, ig_hbm, lsem.at[L_OUT]))
     for copy in outs:
         copy.wait()
 
@@ -403,9 +414,10 @@
             pltpu.VMEM((NSLOT, PACK, 128), BF16),
             pltpu.VMEM((80, F), F32),
             pltpu.VMEM((S, T, CS), F32),
-            pltpu.VMEM((7, S, 32, CS), BF16),
-            pltpu.VMEM((7, S, 32, CS), BF16),
-            pltpu.VMEM((S, 32, CS), BF16),
+            pltpu.VMEM((5, S, 32, CS), BF16),
+            pltpu.VMEM((5, S, 32, CS), BF16),
+            pltpu.VMEM((3, S, 32, CS), BF16),
+            pltpu.VMEM((S, 5, 16, CS), BF16),
             pltpu.VMEM((T // NT, D), BF16),
             pltpu.SemaphoreType.DMA((L_OUT + 3,)),
             pltpu.SemaphoreType.DMA((8,)),

time: 55.6 us -> 52.7 us (0.948)
  the two profiles are of different devices: /device:TPU:4 before, /device:TPU:8 now
where the time goes in v4:
time: 52.7 us; the launch traced here: 52.6 us
  Pallas kernels  50.6 us (96%)
  local copies, waits for them, and re-layouts  1.3 us (2%)
  between operations  0.64 us (1%)
    pallas_call x1, Pallas kernels, per_device(): pl.pallas_call(kernel, out_shape=(jax.ShapeDtypeStruct((T // NT, D), BF16...  50.6 us
    unnamed x2, local copies, waits for them, and re-layouts  1.3 us

profile of v4, /device:TPU:8, one launch (start us, length us, event | category | flops | bytes accessed | tf_op | source)
XLA Modules:
  0.0 52.6 jit_solution(15050194208675014186)
XLA Ops:
  0.6 50.6 %shard_map.59 = (bf16[16,5120]{1,0:T(8,128)(2,1)S(1)}, f32[80,160]{1,0:T(8,128)S(1)}) custom-call(bf16[256,5120]{1,0:T(8,128)(2,1)} %x_hbm.1, bf16[160,5120]{1,0:T(8,128)(2,1)} %w_hbm.1, f32[1,160]{1,0:T(1,128)} %bitcast.1, bf16[160,256]{1,0:T(8,128)(2,1)} %qg_hbm.1), custom_call_target="tpu_custom_call" | custom-call | tf_op jit(solution)/shard_map/pallas_call | solution.py:390
  51.3 0.7 %copy.8 = bf16[16,5120]{1,0:T(8,128)(2,1)} copy(bf16[16,5120]{1,0:T(8,128)(2,1)S(1)} %get-tuple-element.4) | data formatting | bytes 327680
  51.9 0.6 %copy.9 = f32[80,160]{1,0:T(8,128)} copy(f32[80,160]{1,0:T(8,128)S(1)} %get-tuple-element.5) | data formatting | bytes 102400

commit v5 on v4

--- a/solution.py
+++ b/solution.py
@@ -13,17 +13,18 @@
 HALF = D // 2
 S = 4
 CS = HALF // S
-KC = 4
+KC = 8
 KW = D // KC
 HQ = F * NT
 epsilon = 1e-6
 
-PARENT = {8: 7, 7: 5, 6: 5, 5: 0, 4: 3, 3: 1, 2: 1, 1: 0, -7: -5, -6: -5, -5: 0, -4: -3, -3: -1, -2: -1, -1: 0}
-CROSS = {8: 7, 7: 7, 6: 5, 5: 5, -7: -5, -6: -5, -5: -5, 1: 0, -1: 0, 0: 0}
+PARENT = {8: 6, 7: 6, 6: 4, 5: 4, 4: 0, 3: 1, 2: 1, 1: 0, -7: -6, -6: -4, -5: -4, -4: 0, -3: -1, -2: -1, -1: 0}
+CROSS = {8: 6, 7: 6, 6: 6, 5: 4, 4: 4, -7: -6, -6: -6, -5: -4, -4: -4, 1: 0, -1: 0, 0: 0}
 GROUPS = ((8, 7, -7), (6, -6, 5, -5), (4, -4, 3, -3), (2, -2, 1, -1, 0))
 ORDER = sum(GROUPS, ())
 AT = {r: i for i, r in enumerate(ORDER)}
-JOINS = (7, 5, -5, 3, -3, 1, -1, 0)
+JOINS = (6, -6, 4, -4, 1, -1, 0)
+FAR = 4
 SLOT, JOIN_SLOTS = {}, {}
 count = 0
 for j in JOINS:
@@ -31,7 +32,7 @@
     for r in ORDER:
         if PARENT.get(r) == j:
             SLOT["own", r] = count
-            count += 2 if abs(r) < 5 and j else 1
+            count += 2 if abs(r) < FAR and j else 1
         if CROSS.get(r) == j:
             SLOT["cross", r] = count
             count += 1
@@ -115,7 +116,7 @@
     barrier = pltpu.get_barrier_semaphore()
     peers = [{"dp": d, "tensor": lax.rem(t + o, NT)} for o in range(1, NT)]
     peers += [across, sibling]
-    peers += [dev(xh, zat(r), core, xl, y) for r in (1, -1, 2, -2, 5, -5)]
+    peers += [dev(xh, zat(r), core, xl, y) for r in (1, -1, 2, -2, 4, -4)]
     peers += [dev(1 - xh, zat(r), core, xl, y) for r in (0, 1, -1, 2, -2)]
     for p in peers:
         pl.semaphore_signal(barrier, inc=1, device_id=p, device_id_type=MESH)
@@ -237,10 +238,10 @@
         at = pl.ds(AT[GROUPS[g][0]], len(GROUPS[g]))
         arrived(drecv.at[at], DD + g)
         for r in GROUPS[g]:
-            if abs(r) >= 5 or r == 0:
+            if abs(r) >= FAR or r == 0:
                 zcross(r, local(r, 1 - xh))
             if r not in JOINS:
-                if abs(r) >= 5:
+                if abs(r) >= FAR:
                     zown(r, local(r, xh))
                 else:
                     zboth(r, [local(r, h) for h in (0, 1)])
@@ -249,13 +250,13 @@
         first, n = JOIN_SLOTS[r]
         arrived(zrecv.at[pl.ds(first, n)], ZC + JOINS.index(r))
         slots = range(first, first + n)
-        if abs(r) >= 5 or r == 0:
+        if abs(r) >= FAR or r == 0:
             v = local(r, xh)
             for k in slots:
                 v = v + zrecv[k].astype(F32)
             return v
         pair = []
-        for h in ((0, 1) if abs(r) == 3 else (xh, 1 - xh)):
+        for h in (xh, 1 - xh):
             v = local(r, h)
             for k in range(first, first + n, 2):
                 v = v + zrecv[k + h].astype(F32)
@@ -264,10 +265,8 @@
 
     def zjoin(r):
         v = joined(r)
-        if abs(r) == 5 or r == 7:
+        if abs(r) >= FAR:
             zown(r, v)
-        elif abs(r) == 3:
-            zboth(r, v)
         else:
             zcross(r, v[1])
             zown(r, v[0])
@@ -324,7 +323,6 @@
         part_v[s] = dot(own, wst_v[:F, s * CS : (s + 1) * CS], ((1,), (0,)))
     zleaf(0)
     zleaf(1)
-    blocks(2)
     arrived(pgp_v, PG)
     theirs = pgp_v[...].T
     for n in (0, 1):
@@ -335,22 +333,28 @@
         ystep(0, s)
     for s in range(S):
         yown_cross(s)
+    blocks(2)
+    blocks(3)
     zleaf(2)
-    blocks(3)
     zleaf(3)
-    zjoin(7)
-    for s in range(S):
+    for s in (0, 1):
         ystep(1, s)
-    zjoin(3)
-    zjoin(-3)
-    zjoin(-5)
-    zjoin(5)
-    for s in range(S):
+    zjoin(6)
+    zjoin(-6)
+    for s in (2, 3):
+        ystep(1, s)
+    for s in (0, 1):
         ystep(2, s)
-    for s in range(S):
-        ystep(3, s)
+    for s in (2, 3):
+        ystep(2, s)
     zjoin(1)
     zjoin(-1)
+    zjoin(4)
+    zjoin(-4)
+    for s in (0, 1):
+        ystep(3, s)
+    for s in (2, 3):
+        ystep(3, s)
     outs = []
     for s in range(S):
         arrived(yfin.at[s], YF + s)

time: 52.7 us -> 51.6 us (0.979)
  the two profiles are of different devices: /device:TPU:8 before, /device:TPU:1 now
where the time goes in v5:
time: 51.6 us; the launch traced here: 51.5 us
  Pallas kernels  49.5 us (96%)
  local copies, waits for them, and re-layouts  1.3 us (3%)
  between operations  0.64 us (1%)
    pallas_call x1, Pallas kernels, per_device(): pl.pallas_call(kernel, out_shape=(jax.ShapeDtypeStruct((T // NT, D), BF16...  49.5 us
    unnamed x2, local copies, waits for them, and re-layouts  1.3 us

profile of v5, /device:TPU:1, one launch (start us, length us, event | category | flops | bytes accessed | tf_op | source)
XLA Modules:
  0.0 51.5 jit_solution(10206611962813146882)
XLA Ops:
  0.6 49.5 %shard_map.59 = (bf16[16,5120]{1,0:T(8,128)(2,1)S(1)}, f32[80,160]{1,0:T(8,128)S(1)}) custom-call(bf16[256,5120]{1,0:T(8,128)(2,1)} %x_hbm.1, bf16[160,5120]{1,0:T(8,128)(2,1)} %w_hbm.1, f32[1,160]{1,0:T(1,128)} %bitcast.1, bf16[160,256]{1,0:T(8,128)(2,1)} %qg_hbm.1), custom_call_target="tpu_custom_call" | custom-call | tf_op jit(solution)/shard_map/pallas_call | solution.py:394
  50.1 0.7 %copy.8 = bf16[16,5120]{1,0:T(8,128)(2,1)} copy(bf16[16,5120]{1,0:T(8,128)(2,1)S(1)} %get-tuple-element.4) | data formatting | bytes 327680
  50.8 0.6 %copy.9 = f32[80,160]{1,0:T(8,128)} copy(f32[80,160]{1,0:T(8,128)S(1)} %get-tuple-element.5) | data formatting | bytes 102400

commit v6 on v5

--- a/solution.py
+++ b/solution.py
@@ -51,7 +51,7 @@
 YF = YC + 5 * S
 NRECV = YF + S
 S_SUMS, S_WX, S_WD, S_PG, S_DD, S_Z, S_Y, S_YF = range(8)
-L_QG, L_GAIN, L_WH, L_OUT = 2 * KC, 2 * KC + 1, 2 * KC + 2, 2 * KC + 3
+L_QG, L_GAIN, L_WH = KC, KC + 1, KC + 2
 
 
 def dot(a, b, dims):
@@ -67,10 +67,10 @@
 
 
 def kernel(
-    x_hbm, w_hbm, gain_hbm, qg_hbm, ig_hbm, wg_hbm,
-    x_v, xt_v, w_v, wst_v, gain_v, qg_v, sums_v, pga_v, pgp_v, sgt_v, ptt_v,
-    dsend, drecv, own_v, zs_v, zrecv, wg_v,
-    part_v, ysend, yrecv, ylast, yfin, out_v,
+    x_hbm, w_hbm, gain_hbm, qg_hbm, out_v, wg_v,
+    xw_v, xt_v, wst_v, gain_v, qg_v, sums_v, pga_v, pgp_v, sgt_v, ptt_v,
+    dsend, drecv, own_v, zs_v, zrecv,
+    part_v, ysend, yrecv, ylast, yfin,
     lsem, ssem, rsem,
 ):
     d = lax.axis_index("dp")
@@ -95,23 +95,17 @@
     partner = dev(xh, z, core, 1 - xl, y)
     across = dev(1 - xh, z, core, 1 - xl, y)
 
-    loads = []
     for k in range(KC):
         cols = pl.ds(k * KW, KW)
-        loads.append((
-            pltpu.make_async_copy(x_hbm.at[:, cols], x_v.at[:, cols], lsem.at[k]),
-            pltpu.make_async_copy(w_hbm.at[:, cols], w_v.at[:, cols], lsem.at[KC + k]),
-        ))
-    for a, b in loads:
-        a.start()
-        b.start()
+        pltpu.make_async_copy(x_hbm.at[:, cols], xw_v.at[:T, cols], lsem.at[k]).start()
+        pltpu.make_async_copy(w_hbm.at[:, cols], xw_v.at[T:, cols], lsem.at[k]).start()
+    x_v, w_v = xw_v.at[:T], xw_v.at[T:]
     qg_load = pltpu.make_async_copy(qg_hbm, qg_v, lsem.at[L_QG])
     qg_load.start()
     gain_load = pltpu.make_async_copy(gain_hbm, gain_v, lsem.at[L_GAIN])
     gain_load.start()
     myhalf = pl.ds(pl.multiple_of(xl * HALF, 128), HALF)
     wh_load = pltpu.make_async_copy(w_hbm.at[:, myhalf], wst_v.at[:F], lsem.at[L_WH])
-    wh_load.start()
 
     barrier = pltpu.get_barrier_semaphore()
     peers = [{"dp": d, "tensor": lax.rem(t + o, NT)} for o in range(1, NT)]
@@ -122,12 +116,16 @@
         pl.semaphore_signal(barrier, inc=1, device_id=p, device_id_type=MESH)
 
     pt = None
-    for k, (a, b) in enumerate(loads):
-        a.wait()
-        b.wait()
+    for k in range(KC):
         cols = slice(k * KW, (k + 1) * KW)
-        term = dot(w_v[:, cols], x_v[:, cols], ((1,), (1,)))
+        pltpu.make_async_copy(xw_v.at[:, cols], xw_v.at[:, cols], lsem.at[k]).wait()
+        turned = x_v[:, cols].T
+        h = k * KW // HALF
+        for i in range(KW // 160):
+            xt_v[k * KW % HALF // 160 + i, h * 160 : h * 160 + 160, :] = turned[i * 160 : i * 160 + 160]
+        term = dot(w_v[:, cols], turned, ((1,), (0,)))
         pt = term if pt is None else pt + term
+    wh_load.start()
     qg_load.wait()
     gain_load.wait()
     rows = lax.broadcasted_iota(jnp.int32, (F, F), 0)
@@ -170,14 +168,6 @@
         dst = pl.ds(pl.multiple_of((2 * n + core) * CS, 128), CS)
         send(w_v.at[:, src], wpart.at[:, dst], S_WX, WX + n, who)
 
-    for k in range(D // 256):
-        turned = x_v[:, k * 256 : (k + 1) * 256].T
-        at, end = k * 256, (k + 1) * 256
-        while at < end:
-            h, zz, o = at // HALF, at % HALF // 160, at % 160
-            n = min(160 - o, end - at)
-            xt_v[zz, h * 160 + o : h * 160 + o + n, :] = turned[at - k * 256 : at - k * 256 + n]
-            at += n
     pga_v[F:, :] = jnp.zeros((256 - F, T), BF16)
     sgt_v[...] = sg.T
     ptt_v[...] = pt.T
@@ -310,26 +300,25 @@
         ylast_send(3, s, ylast.at[2, s], None)
 
     blocks(0)
-    blocks(1)
     for n in (0, 1):
         cols = pl.ds(pl.multiple_of((2 * n + core) * CS, 128), CS)
         arrived(wpart.at[:, cols], WX + n)
         send(wpart.at[:, cols], wpart.at[:, cols], S_WD, WD + n, sibling)
     wh_load.wait()
+    blocks(1)
+    zleaf(0)
     both = jnp.concatenate([inv, coef], axis=0)
     both = jnp.concatenate([both, jnp.zeros((6, T), F32)], axis=0).T
     own = (both[:, 0:1] * sgt_v[...] - both[:, 1:2] * ptt_v[...]).astype(BF16)
     for s in range(S):
         part_v[s] = dot(own, wst_v[:F, s * CS : (s + 1) * CS], ((1,), (0,)))
-    zleaf(0)
     zleaf(1)
     arrived(pgp_v, PG)
-    theirs = pgp_v[...].T
     for n in (0, 1):
         cols = pl.ds(pl.multiple_of((2 * n + 1 - core) * CS, 128), CS)
         arrived(wpart.at[:, cols], WD + n)
     for s in range(S):
-        part_v[s] += dot(theirs, wst_v[F:, s * CS : (s + 1) * CS], ((1,), (0,)))
+        part_v[s] += dot(pgp_v[...], wst_v[F:, s * CS : (s + 1) * CS], ((0,), (0,)))
         ystep(0, s)
     for s in range(S):
         yown_cross(s)
@@ -339,10 +328,10 @@
     zleaf(3)
     for s in (0, 1):
         ystep(1, s)
+    for s in (2, 3):
+        ystep(1, s)
     zjoin(6)
     zjoin(-6)
-    for s in (2, 3):
-        ystep(1, s)
     for s in (0, 1):
         ystep(2, s)
     for s in (2, 3):
@@ -355,7 +344,6 @@
         ystep(3, s)
     for s in (2, 3):
         ystep(3, s)
-    outs = []
     for s in range(S):
         arrived(yfin.at[s], YF + s)
         own = part_v[s, pl.ds(yrows(0) + xl * 128, 16), :]
@@ -364,7 +352,6 @@
                 v = v + yfin[s, slot].astype(F32)
             cols = pl.ds(pl.multiple_of(who * HALF + s * CS, 128), CS)
             out_v[:, cols] = v.astype(BF16)
-            pltpu.make_async_copy(out_v.at[:, cols], ig_hbm.at[:, cols], lsem.at[L_OUT]).start()
 
     v = joined(0)
     wg_v[:, :128] = v[:80]
@@ -372,8 +359,6 @@
     for j in (1, 2, 3):
         wg_v[16 * j : 16 * j + 16, 128:] = pltpu.roll(v[80:96], 128 - 32 * j, 1)[:, :32]
     wg_v[64:, 128:] = v[96:, :32]
-    outs.append(pltpu.make_async_copy(wg_v, wg_hbm, lsem.at[L_OUT + 1]))
-    outs[0].start()
 
     left(sums_v.at[: NT - 1], S_SUMS)
     left(wpart.at[:, : 2 * CS], S_WX)
@@ -383,26 +368,20 @@
     left(zrecv, S_Z)
     left(yrecv, S_Y)
     left(yfin, S_YF)
-    outs.append(pltpu.make_async_copy(out_v, ig_hbm, lsem.at[L_OUT]))
-    for copy in outs:
-        copy.wait()
 
 
 def per_device(block_input, query_weight, query_gain, query_grad):
     hbm = pl.BlockSpec(memory_space=pltpu.HBM)
-    anywhere = pl.BlockSpec(memory_space=pl.ANY)
+    vmem = pl.BlockSpec(memory_space=pltpu.VMEM)
+    outs = (jax.ShapeDtypeStruct((T // NT, D), BF16), jax.ShapeDtypeStruct((80, F), F32))
     return pl.pallas_call(
         kernel,
-        out_shape=(
-            jax.ShapeDtypeStruct((T // NT, D), BF16),
-            jax.ShapeDtypeStruct((80, F), F32),
-        ),
+        out_shape=outs,
         in_specs=[hbm, hbm, hbm, hbm],
-        out_specs=(anywhere, anywhere),
+        out_specs=(vmem, vmem),
         scratch_shapes=[
-            pltpu.VMEM((T, D), BF16),
+            pltpu.VMEM((T + F, D), BF16),
             pltpu.VMEM((NZ, 320, T), BF16),
-            pltpu.VMEM((F, D), BF16),
             pltpu.VMEM((2 * F, HALF), BF16),
             pltpu.VMEM((1, F), F32),
             pltpu.VMEM((F, T), BF16),
@@ -416,14 +395,12 @@
             pltpu.VMEM((16, 2, PACK, 128), F32),
             pltpu.VMEM((16, 2, PACK, 128), BF16),
             pltpu.VMEM((NSLOT, PACK, 128), BF16),
-            pltpu.VMEM((80, F), F32),
             pltpu.VMEM((S, T, CS), F32),
             pltpu.VMEM((5, S, 32, CS), BF16),
             pltpu.VMEM((5, S, 32, CS), BF16),
             pltpu.VMEM((3, S, 32, CS), BF16),
             pltpu.VMEM((S, 5, 16, CS), BF16),
-            pltpu.VMEM((T // NT, D), BF16),
-            pltpu.SemaphoreType.DMA((L_OUT + 3,)),
+            pltpu.SemaphoreType.DMA((KC + 3,)),
             pltpu.SemaphoreType.DMA((8,)),
             pltpu.SemaphoreType.DMA((NRECV,)),
         ],

time: 51.6 us -> 50.6 us (0.981)
  Pallas kernels: 49.5 us -> 48.5 us
    pallas_call x1, Pallas kernels: 49.5 us -> 48.5 us  [per_device(): pl.pallas_call(kernel, out_shape=outs, in_specs=[hbm, hbm, hbm, hbm], out...]
where the time goes in v6:
time: 50.6 us; the launch traced here: 50.4 us
  Pallas kernels  48.5 us (96%)
  local copies, waits for them, and re-layouts  1.3 us (3%)
  between operations  0.64 us (1%)
    pallas_call x1, Pallas kernels, per_device(): pl.pallas_call(kernel, out_shape=outs, in_specs=[hbm, hbm, hbm, hbm], out...  48.5 us
    unnamed x2, local copies, waits for them, and re-layouts  1.3 us

profile of v6, /device:TPU:1, one launch (start us, length us, event | category | flops | bytes accessed | tf_op | source)
XLA Modules:
  0.0 50.4 jit_solution(17025734524912908141)
XLA Ops:
  0.6 48.5 %shard_map.59 = (bf16[16,5120]{1,0:T(8,128)(2,1)S(1)}, f32[80,160]{1,0:T(8,128)S(1)}) custom-call(bf16[256,5120]{1,0:T(8,128)(2,1)} %x_hbm.1, bf16[160,5120]{1,0:T(8,128)(2,1)} %w_hbm.1, f32[1,160]{1,0:T(1,128)} %bitcast.1, bf16[160,256]{1,0:T(8,128)(2,1)} %qg_hbm.1), custom_call_target="tpu_custom_call" | custom-call | tf_op jit(solution)/shard_map/pallas_call | solution.py:377
  49.1 0.7 %copy.8 = bf16[16,5120]{1,0:T(8,128)(2,1)} copy(bf16[16,5120]{1,0:T(8,128)(2,1)S(1)} %get-tuple-element.4) | data formatting | bytes 327680
  49.8 0.6 %copy.9 = f32[80,160]{1,0:T(8,128)} copy(f32[80,160]{1,0:T(8,128)S(1)} %get-tuple-element.5) | data formatting | bytes 102400

commit v7 on v6

--- a/solution.py
+++ b/solution.py
@@ -11,8 +11,9 @@
 NT, NY, NZ = 16, 8, 16
 T, F, D = 256, 160, 5120
 HALF = D // 2
-S = 4
+S = 5
 CS = HALF // S
+WS = HALF // 4
 KC = 8
 KW = D // KC
 HQ = F * NT
@@ -164,8 +165,8 @@
 
     wpart = wst_v.at[F:]
     for n, who in enumerate((partner, across)):
-        src = pl.ds(pl.multiple_of((1 - xl) * HALF + (2 * n + core) * CS, 128), CS)
-        dst = pl.ds(pl.multiple_of((2 * n + core) * CS, 128), CS)
+        src = pl.ds(pl.multiple_of((1 - xl) * HALF + (2 * n + core) * WS, 128), WS)
+        dst = pl.ds(pl.multiple_of((2 * n + core) * WS, 128), WS)
         send(w_v.at[:, src], wpart.at[:, dst], S_WX, WX + n, who)
 
     pga_v[F:, :] = jnp.zeros((256 - F, T), BF16)
@@ -301,7 +302,7 @@
 
     blocks(0)
     for n in (0, 1):
-        cols = pl.ds(pl.multiple_of((2 * n + core) * CS, 128), CS)
+        cols = pl.ds(pl.multiple_of((2 * n + core) * WS, 128), WS)
         arrived(wpart.at[:, cols], WX + n)
         send(wpart.at[:, cols], wpart.at[:, cols], S_WD, WD + n, sibling)
     wh_load.wait()
@@ -315,7 +316,7 @@
     zleaf(1)
     arrived(pgp_v, PG)
     for n in (0, 1):
-        cols = pl.ds(pl.multiple_of((2 * n + 1 - core) * CS, 128), CS)
+        cols = pl.ds(pl.multiple_of((2 * n + 1 - core) * WS, 128), WS)
         arrived(wpart.at[:, cols], WD + n)
     for s in range(S):
         part_v[s] += dot(pgp_v[...], wst_v[F:, s * CS : (s + 1) * CS], ((0,), (0,)))
@@ -328,13 +329,13 @@
     zleaf(3)
     for s in (0, 1):
         ystep(1, s)
-    for s in (2, 3):
+    for s in (2, 3, 4):
         ystep(1, s)
     zjoin(6)
     zjoin(-6)
     for s in (0, 1):
         ystep(2, s)
-    for s in (2, 3):
+    for s in (2, 3, 4):
         ystep(2, s)
     zjoin(1)
     zjoin(-1)
@@ -342,7 +343,7 @@
     zjoin(-4)
     for s in (0, 1):
         ystep(3, s)
-    for s in (2, 3):
+    for s in (2, 3, 4):
         ystep(3, s)
     for s in range(S):
         arrived(yfin.at[s], YF + s)
@@ -361,8 +362,8 @@
     wg_v[64:, 128:] = v[96:, :32]
 
     left(sums_v.at[: NT - 1], S_SUMS)
-    left(wpart.at[:, : 2 * CS], S_WX)
-    left(wpart.at[:, : 2 * CS], S_WD)
+    left(wpart.at[:, : 2 * WS], S_WX)
+    left(wpart.at[:, : 2 * WS], S_WD)
     left(pgp_v, S_PG)
     left(dsend, S_DD)
     left(zrecv, S_Z)

time: 50.6 us -> 51.1 us (level)
  no operation moved by 1% of the time
where the time goes in v7:
time: 51.1 us; the launch traced here: 50.9 us
  Pallas kernels  49 us (96%)
  local copies, waits for them, and re-layouts  1.3 us (3%)
  between operations  0.64 us (1%)
    pallas_call x1, Pallas kernels, per_device(): pl.pallas_call(kernel, out_shape=outs, in_specs=[hbm, hbm, hbm, hbm], out...  49 us
    unnamed x2, local copies, waits for them, and re-layouts  1.3 us

profile of v7, /device:TPU:1, one launch (start us, length us, event | category | flops | bytes accessed | tf_op | source)
XLA Modules:
  0.0 50.9 jit_solution(9926123871496720941)
XLA Ops:
  0.6 49.0 %shard_map.59 = (bf16[16,5120]{1,0:T(8,128)(2,1)S(1)}, f32[80,160]{1,0:T(8,128)S(1)}) custom-call(bf16[256,5120]{1,0:T(8,128)(2,1)} %x_hbm.1, bf16[160,5120]{1,0:T(8,128)(2,1)} %w_hbm.1, f32[1,160]{1,0:T(1,128)} %bitcast.1, bf16[160,256]{1,0:T(8,128)(2,1)} %qg_hbm.1), custom_call_target="tpu_custom_call" | custom-call | tf_op jit(solution)/shard_map/pallas_call | solution.py:378
  49.6 0.7 %copy.8 = bf16[16,5120]{1,0:T(8,128)(2,1)} copy(bf16[16,5120]{1,0:T(8,128)(2,1)S(1)} %get-tuple-element.4) | data formatting | bytes 327680
  50.3 0.6 %copy.9 = f32[80,160]{1,0:T(8,128)} copy(f32[80,160]{1,0:T(8,128)S(1)} %get-tuple-element.5) | data formatting | bytes 102400

commit v8 on v6

--- a/solution.py
+++ b/solution.py
@@ -320,12 +320,12 @@
     for s in range(S):
         part_v[s] += dot(pgp_v[...], wst_v[F:, s * CS : (s + 1) * CS], ((0,), (0,)))
         ystep(0, s)
-    for s in range(S):
-        yown_cross(s)
     blocks(2)
     blocks(3)
     zleaf(2)
     zleaf(3)
+    for s in range(S):
+        yown_cross(s)
     for s in (0, 1):
         ystep(1, s)
     for s in (2, 3):

time: 50.6 us -> 50.3 us (level)
  no operation moved by 1% of the time
where the time goes in v8:
time: 50.3 us; the launch traced here: 50 us
  Pallas kernels  48 us (95%)
  local copies, waits for them, and re-layouts  1.3 us (3%)
  between operations  0.64 us (1%)
    pallas_call x1, Pallas kernels, per_device(): pl.pallas_call(kernel, out_shape=outs, in_specs=[hbm, hbm, hbm, hbm], out...  48 us
    unnamed x2, local copies, waits for them, and re-layouts  1.3 us

profile of v8, /device:TPU:1, one launch (start us, length us, event | category | flops | bytes accessed | tf_op | source)
XLA Modules:
  0.0 50.0 jit_solution(12593172302636049171)
XLA Ops:
  0.6 48.0 %shard_map.59 = (bf16[16,5120]{1,0:T(8,128)(2,1)S(1)}, f32[80,160]{1,0:T(8,128)S(1)}) custom-call(bf16[256,5120]{1,0:T(8,128)(2,1)} %x_hbm.1, bf16[160,5120]{1,0:T(8,128)(2,1)} %w_hbm.1, f32[1,160]{1,0:T(1,128)} %bitcast.1, bf16[160,256]{1,0:T(8,128)(2,1)} %qg_hbm.1), custom_call_target="tpu_custom_call" | custom-call | tf_op jit(solution)/shard_map/pallas_call | solution.py:377
  48.7 0.7 %copy.8 = bf16[16,5120]{1,0:T(8,128)(2,1)} copy(bf16[16,5120]{1,0:T(8,128)(2,1)S(1)} %get-tuple-element.4) | data formatting | bytes 327680
  49.3 0.6 %copy.9 = f32[80,160]{1,0:T(8,128)} copy(f32[80,160]{1,0:T(8,128)S(1)} %get-tuple-element.5) | data formatting | bytes 102400
